TPU v7x, 32 devices: a whole 2x2x4 slice. The times are simulated.
32 devices in a mesh: depth: 8 (over y, x, core), plane: 4 (over z).
Axes of the slice: x: 2, y: 2, z: 4, core: 2. Of those that a mesh axis runs over, the one named last changes fastest.
Arguments:
- activations: bfloat16 [8, 8, 64, 1024], P('plane', 'depth'), may hold values from -6 to 6
- plane_weight: bfloat16 [2, 3, 64, 576], replicated, may hold values from -0.375 to 0.375
- plane_bias: float32 [2, 3, 64], replicated, may hold values from -3 to 3
- depth_weight: bfloat16 [2, 64, 192], replicated, may hold values from -0.75 to 0.75
- depth_bias: float32 [2, 64], replicated, may hold values from -3 to 3
- counts: int32 [4], replicated, may hold values from 1 to 2, as said below
- neighbours: int32 [8, 8], P('plane'), may hold values from -1 to 7, as said below
- voxel_mask: int32 [8, 8, 1024], P('plane', 'depth'), may hold values from 0 to 1, as said below
Outputs:
- hidden: bfloat16 [8, 8, 64, 1024], P('plane', 'depth')
Inputs may be any that keep to these rules, and one draw needn't show every extreme that they name: `counts`: each entry is between 1 and 2; at least one entry equals 2. `neighbours`: for a live slot, the live slot that holds the adjacent tile of a grid in that direction, or -1; all -1 for dead slots; neighbourhood is symmetric. `voxel_mask`: zero in dead slots.
All inputs are finite; a program needn't handle non-finite values.
Results may differ from a plain program's by a relative error of at most 0.008.
Values may be sent and summed in bfloat16 or wider, within the bound.
No kernel may reach another device: no remote copies, remote signals or barrier semaphores. Data moves between devices by JAX's collectives and lax.ppermute only.
A program may use at most 64 MiB of HBM per device.

v0:
```python
import jax
import jax.numpy as jnp
from jax import lax
from jax.sharding import PartitionSpec as P

TILE = 32
BLOCKS = 2


def with_halo(cells, sides, width):
    for axis, dim in sides:
        count = lax.axis_size(axis)
        ends = count - 1
        head = lax.slice_in_dim(cells, 0, width, axis=dim)
        tail = lax.slice_in_dim(cells, cells.shape[dim] - width, cells.shape[dim], axis=dim)
        cells = jnp.concatenate(
            [
                lax.ppermute(tail, axis, [(i, (i + 1) % count) for i in range(ends)]),
                cells,
                lax.ppermute(head, axis, [((i + 1) % count, i) for i in range(ends)]),
            ],
            axis=dim,
        )
    return cells


def flatten(array):
    return array.reshape(array.shape[:-2] + (-1,))


def strips(tile_view, strip_width):
    top_rows = tile_view[..., :strip_width, :]
    bottom = tile_view[..., TILE - strip_width :, :]
    left_cols = tile_view[..., :, :strip_width]
    right_cols = tile_view[..., :, TILE - strip_width :]
    return jnp.concatenate(
        [flatten(top_rows), flatten(bottom), flatten(left_cols), flatten(right_cols)], -1
    )


def surround(center, neighbour_table, strip_pool, strip_width):
    length = strip_width * TILE
    present = neighbour_table >= 0
    safe_index = jnp.maximum(neighbour_table, 0)

    def fetch_strip(column, segment, piece_shape):
        pieces = strip_pool[safe_index[:, column]][..., segment * length : (segment + 1) * length]
        pieces = pieces.reshape(pieces.shape[:-1] + piece_shape)
        keep = present[:, column].reshape((-1,) + (1,) * (pieces.ndim - 1))
        return jnp.where(keep, pieces, jnp.zeros_like(pieces))

    rows_shape = (strip_width, TILE)
    cols_shape = (TILE, strip_width)
    north_west = fetch_strip(0, 1, rows_shape)[..., TILE - strip_width :]
    north = fetch_strip(1, 1, rows_shape)
    north_east = fetch_strip(2, 1, rows_shape)[..., :strip_width]
    west_side = fetch_strip(3, 3, cols_shape)
    east_side = fetch_strip(4, 2, cols_shape)
    south_west = fetch_strip(5, 0, rows_shape)[..., TILE - strip_width :]
    south_side = fetch_strip(6, 0, rows_shape)
    south_east = fetch_strip(7, 0, rows_shape)[..., :strip_width]
    upper_band = jnp.concatenate([north_west, north, north_east], -1)
    middle = jnp.concatenate([west_side, center, east_side], -1)
    lower_band = jnp.concatenate([south_west, south_side, south_east], -1)
    return jnp.concatenate([upper_band, middle, lower_band], -2)


def plane_conv(padded, weight):
    side = padded.shape[-1]
    inner = side - 2
    span = inner * side
    length = -(-span // 128) * 128
    flat = padded.reshape(padded.shape[:-2] + (side * side,))
    extra = length + 2 * side + 2 - side * side
    flat = jnp.pad(flat, [(0, 0)] * (flat.ndim - 1) + [(0, extra)])
    channels = weight.shape[0]
    total = None
    for row_off in range(3):
        for col_off in range(3):
            tap = row_off * 3 + col_off
            start = row_off * side + col_off
            view = flat[..., start : start + length]
            term = jnp.einsum(
                "ok,nskq->nsoq",
                weight[:, tap * channels : (tap + 1) * channels],
                view,
                preferred_element_type=jnp.float32,
            )
            total = term if total is None else total + term
    result = total[..., :span].reshape(total.shape[:-1] + (inner, side))[..., :inner]
    return result.reshape(result.shape[:-2] + (inner * inner,))


def activate(summed, offsets, layer_mask):
    return (layer_mask * jax.nn.silu(summed + offsets[:, None])).astype(jnp.bfloat16)


def shards(
    activations, plane_weight, plane_bias, depth_weight, depth_bias, counts, neighbours, voxel_mask
):
    slots = activations.shape[0]
    owner_id = lax.axis_index("plane")
    own_count = jnp.sum(
        jnp.where(jnp.arange(counts.shape[0], dtype=jnp.int32) == owner_id, counts, 0)
    )
    alive = jnp.arange(slots, dtype=jnp.int32) < own_count
    hidden = jnp.where(alive[:, None, None, None], activations, jnp.zeros_like(activations))
    mask_f = voxel_mask.astype(jnp.float32)[:, :, None, :]
    mask_tiles = voxel_mask.reshape(voxel_mask.shape[:-1] + (TILE, TILE))
    mask_pool = lax.all_gather(strips(mask_tiles, 2), "plane", axis=0, tiled=True)
    mask_wide = surround(mask_tiles, neighbours, mask_pool, 2).astype(jnp.float32)[:, :, None]
    for block_id in range(BLOCKS):
        tiles_view = hidden.reshape(hidden.shape[:-1] + (TILE, TILE))
        wide_pool = lax.all_gather(strips(tiles_view, 3), "plane", axis=0, tiled=True)
        padded = surround(tiles_view, neighbours, wide_pool, 3)
        for layer_id in range(3):
            summed = plane_conv(padded, plane_weight[block_id, layer_id])
            inner = padded.shape[-1] - 2
            margin = (mask_wide.shape[-1] - inner) // 2
            layer_mask = mask_wide[..., margin : margin + inner, margin : margin + inner]
            layer_mask = layer_mask.reshape(layer_mask.shape[:-2] + (inner * inner,))
            padded = activate(summed, plane_bias[block_id, layer_id], layer_mask).reshape(
                summed.shape[:-1] + (inner, inner)
            )
        branch = padded.reshape(hidden.shape)
        extended = with_halo(branch, (("depth", 1),), 1)
        stacked = jnp.concatenate([extended[:, :-2], extended[:, 1:-1], extended[:, 2:]], axis=2)
        summed = jnp.einsum(
            "ok,nskq->nsoq", depth_weight[block_id], stacked, preferred_element_type=jnp.float32
        )
        hidden = (
            hidden.astype(jnp.float32) + mask_f * (summed + depth_bias[block_id][:, None])
        ).astype(jnp.bfloat16)
    return hidden


def solution(mesh):
    in_specs = (
        P("plane", "depth", None, None),
        P(),
        P(),
        P(),
        P(),
        P(),
        P("plane", None),
        P("plane", "depth", None),
    )
    out_specs = P("plane", "depth", None, None)
    return jax.shard_map(shards, mesh=mesh, in_specs=in_specs, out_specs=out_specs, check_vma=False)
```

profile of v0, /device:TPU:3, one launch (start us, length us, event | category | flops | bytes accessed | tf_op | source)
XLA Modules:
  0.0 131.7 jit_solution(11813996449193607016)
XLA Ops:
  0.0 1.3 %fusion.151 = s32[]{:T(128)} fusion(s32[4]{0:T(128)} %param.13, s32[]{:T(128)S(6)} %axis_index.12), kind=kLoop, calls=%fused_computation.373 | loop fusion | flops 11 | bytes 24 | tf_op jit(solution)/shard_map/reduce_sum | solution.py:103
  2.0 1.0 bitcast_select_fusion
  4.0 13.1 %all_gather.10 = bf16[8,1,64,384]{3,2,1,0:T(8,128)(2,1)S(1)} all-gather(bf16[2,1,64,384]{3,2,1,0:T(8,128)(2,1)S(1)} %copy.109), channel_id=1, replica_groups=mesh['depth'=8,'plane'=4] {'plane'}, dimensions={0}, use_global_device_ids=true | all-gather | bytes 491520 | tf_op jit(solution)/shard_map/all_gather | solution.py:114
  19.0 9.3 %all_gather.9 = s32[8,1,256]{2,1,0:T(1,128)S(1)} all-gather(s32[2,1,256]{2,1,0:T(1,128)S(1)} %copy.103), channel_id=1, replica_groups=mesh['depth'=8,'plane'=4] {'plane'}, dimensions={0}, use_global_device_ids=true | all-gather | bytes 10240 | tf_op jit(solution)/shard_map/all_gather | solution.py:110
  47.8 1.0 copy.125
  48.9 1.6 %copy.126 = f32[2,1,64,1296]{3,2,0,1:T(8,128)S(1)} copy(f32[2,1,64,1296]{2,0,3,1:T(2,128)S(1)} %bitcast.566) | data formatting | bytes 1327104 | tf_op jit(solution)/shard_map/reshape | solution.py:91
  54.3 1.1 copy.127
  55.5 1.0 copy.128
  59.7 1.1 copy.129
  61.9 8.3 %collective-permute-start = (bf16[2,1,64,1024]{3,2,0,1:T(8,128)(2,1)S(1)}, bf16[2,1,64,1024]{3,2,0,1:T(8,128)(2,1)S(1)}, u32[]{:S(2)}, u32[]{:S(2)}) collective-permute-start(bf16[2,1,64,1024]{3,2,0,1:T(8,128)(2,1)S(1)} %multiply_convert_fusion.5), channel_id=1, source_target_pairs={{0,4},{4,8},{8,12},{12,16},{16,20},{20,24},{24,28},{1,5},{5,9},{9,... | collective-permute-start | bytes 786440 | tf_op jit(solution)/shard_map/ppermute | solution.py:18
  70.2 1.9 %collective-permute-start.1 = (bf16[2,1,64,1024]{3,2,0,1:T(8,128)(2,1)S(1)}, bf16[2,1,64,1024]{3,2,0,1:T(8,128)(2,1)S(1)}, u32[]{:S(2)}, u32[]{:S(2)}) collective-permute-start(bf16[2,1,64,1024]{3,2,0,1:T(8,128)(2,1)S(1)} %multiply_convert_fusion.5), channel_id=1, source_target_pairs={{4,0},{8,4},{12,8},{16,12},{20,16},{24,20},{28,24},{5,1},{9,5},{13... | collective-permute-start | bytes 786440 | tf_op jit(solution)/shard_map/ppermute | solution.py:20
  72.1 1.3 %collective-permute-done = bf16[2,1,64,1024]{3,2,0,1:T(8,128)(2,1)S(1)} collective-permute-done((bf16[2,1,64,1024]{3,2,0,1:T(8,128)(2,1)S(1)}, bf16[2,1,64,1024]{3,2,0,1:T(8,128)(2,1)S(1)}, u32[]{:S(2)}, u32[]{:S(2)}) %collective-permute-start) | collective-permute-done | bytes 262176 | tf_op jit(solution)/shard_map/ppermute | solution.py:18
  73.5 5.3 %collective-permute-done.1 = bf16[2,1,64,1024]{3,2,0,1:T(8,128)(2,1)S(1)} collective-permute-done((bf16[2,1,64,1024]{3,2,0,1:T(8,128)(2,1)S(1)}, bf16[2,1,64,1024]{3,2,0,1:T(8,128)(2,1)S(1)}, u32[]{:S(2)}, u32[]{:S(2)}) %collective-permute-start.1) | collective-permute-done | bytes 262176 | tf_op jit(solution)/shard_map/ppermute | solution.py:20
  80.0 12.9 %all_gather.11 = bf16[8,1,64,384]{3,2,1,0:T(8,128)(2,1)S(1)} all-gather(bf16[2,1,64,384]{3,2,1,0:T(8,128)(2,1)S(1)} %copy.137), channel_id=1, replica_groups=mesh['depth'=8,'plane'=4] {'plane'}, dimensions={0}, use_global_device_ids=true | all-gather | bytes 491520 | tf_op jit(solution)/shard_map/all_gather | solution.py:114
  105.2 1.0 copy.153
  106.2 1.4 %copy.154 = f32[2,1,64,1296]{3,2,0,1:T(8,128)S(1)} copy(f32[2,1,64,1296]{2,0,3,1:T(2,128)S(1)} %bitcast.567) | data formatting | bytes 1327104 | tf_op jit(solution)/shard_map/reshape | solution.py:91
  110.7 1.1 copy.155
  112.0 1.0 copy.156
  116.0 1.1 copy.157
  118.0 4.2 %collective-permute-start.2 = (bf16[2,1,64,1024]{3,2,0,1:T(8,128)(2,1)S(1)}, bf16[2,1,64,1024]{3,2,0,1:T(8,128)(2,1)S(1)}, u32[]{:S(2)}, u32[]{:S(2)}) collective-permute-start(bf16[2,1,64,1024]{3,2,0,1:T(8,128)(2,1)S(1)} %multiply_convert_fusion.4), channel_id=1, source_target_pairs={{0,4},{4,8},{8,12},{12,16},{16,20},{20,24},{24,28},{1,5},{5,9},{9,... | collective-permute-start | bytes 786440 | tf_op jit(solution)/shard_map/ppermute | solution.py:18
  122.2 1.9 %collective-permute-start.3 = (bf16[2,1,64,1024]{3,2,0,1:T(8,128)(2,1)S(1)}, bf16[2,1,64,1024]{3,2,0,1:T(8,128)(2,1)S(1)}, u32[]{:S(2)}, u32[]{:S(2)}) collective-permute-start(bf16[2,1,64,1024]{3,2,0,1:T(8,128)(2,1)S(1)} %multiply_convert_fusion.4), channel_id=1, source_target_pairs={{4,0},{8,4},{12,8},{16,12},{20,16},{24,20},{28,24},{5,1},{9,5},{13... | collective-permute-start | bytes 786440 | tf_op jit(solution)/shard_map/ppermute | solution.py:20
  124.1 2.4 %collective-permute-done.2 = bf16[2,1,64,1024]{3,2,0,1:T(8,128)(2,1)S(1)} collective-permute-done((bf16[2,1,64,1024]{3,2,0,1:T(8,128)(2,1)S(1)}, bf16[2,1,64,1024]{3,2,0,1:T(8,128)(2,1)S(1)}, u32[]{:S(2)}, u32[]{:S(2)}) %collective-permute-start.2) | collective-permute-done | bytes 262176 | tf_op jit(solution)/shard_map/ppermute | solution.py:18
  126.5 4.3 %collective-permute-done.3 = bf16[2,1,64,1024]{3,2,0,1:T(8,128)(2,1)S(1)} collective-permute-done((bf16[2,1,64,1024]{3,2,0,1:T(8,128)(2,1)S(1)}, bf16[2,1,64,1024]{3,2,0,1:T(8,128)(2,1)S(1)}, u32[]{:S(2)}, u32[]{:S(2)}) %collective-permute-start.3) | collective-permute-done | bytes 262176 | tf_op jit(solution)/shard_map/ppermute | solution.py:20
  130.8 1.0 fusion.16
  (307 shorter events, 50.3 us)
Async XLA Ops:
  17.4 20.4 %copy-start.25 = (s32[1024]{0:T(1024)}, s32[1024]{0:T(1024)S(1)}, u32[]{:S(2)}) copy-start(s32[1024]{0:T(1024)S(1)} %get-tuple-element.51) | copy-start | bytes 12292
  17.4 20.4 %copy-start.27 = (s32[1024]{0:T(1024)}, s32[1024]{0:T(1024)S(1)}, u32[]{:S(2)}) copy-start(s32[1024]{0:T(1024)S(1)} %get-tuple-element.52) | copy-start | bytes 12292
  18.0 19.8 %copy-start.26 = (s32[1024]{0:T(1024)}, s32[1024]{0:T(1024)S(1)}, u32[]{:S(2)}) copy-start(s32[1024]{0:T(1024)S(1)} %get-tuple-element.54) | copy-start | bytes 12292
  18.0 19.8 %copy-start.28 = (s32[1024]{0:T(1024)}, s32[1024]{0:T(1024)S(1)}, u32[]{:S(2)}) copy-start(s32[1024]{0:T(1024)S(1)} %get-tuple-element.53) | copy-start | bytes 12292
  29.5 8.3 %copy-start.29 = (s32[1024]{0:T(1024)}, s32[1024]{0:T(1024)S(1)}, u32[]{:S(2)}) copy-start(s32[1024]{0:T(1024)S(1)} %get-tuple-element.49) | copy-start | bytes 12292
  29.5 8.3 %copy-start.30 = (s32[1024]{0:T(1024)}, s32[1024]{0:T(1024)S(1)}, u32[]{:S(2)}) copy-start(s32[1024]{0:T(1024)S(1)} %get-tuple-element.50) | copy-start | bytes 12292
  30.7 7.1 %copy-start.31 = (s32[1024]{0:T(1024)}, s32[1024]{0:T(1024)S(1)}, u32[]{:S(2)}) copy-start(s32[1024]{0:T(1024)S(1)} %get-tuple-element.56) | copy-start | bytes 12292
  30.7 7.1 %copy-start.32 = (s32[1024]{0:T(1024)}, s32[1024]{0:T(1024)S(1)}, u32[]{:S(2)}) copy-start(s32[1024]{0:T(1024)S(1)} %get-tuple-element.55) | copy-start | bytes 12292
  36.7 6.6 %copy-start.17 = (pred[2]{0:T(512)(128)(4,1)}, pred[2]{0:T(512)(128)(4,1)S(1)}, u32[]{:S(2)}) copy-start(pred[2]{0:T(512)(128)(4,1)S(1)} %get-tuple-element.14) | copy-start | bytes 10
  60.9 11.2 %copy-start.38 = (f32[2,64]{1,0:T(2,128)S(1)}, f32[2,64]{1,0:T(2,128)}, u32[]{:S(2)}) copy-start(f32[2,64]{1,0:T(2,128)} %param.12) | copy-start | bytes 1540
  60.9 17.8 %copy-start.39 = (bf16[2,64,192]{2,1,0:T(8,128)(2,1)S(1)}, bf16[2,64,192]{2,1,0:T(8,128)(2,1)}, u32[]{:S(2)}) copy-start(bf16[2,64,192]{2,1,0:T(8,128)(2,1)} %param.11) | copy-start | bytes 147460
  61.9 11.6 %collective-permute-start = (bf16[2,1,64,1024]{3,2,0,1:T(8,128)(2,1)S(1)}, bf16[2,1,64,1024]{3,2,0,1:T(8,128)(2,1)S(1)}, u32[]{:S(2)}, u32[]{:S(2)}) collective-permute-start(bf16[2,1,64,1024]{3,2,0,1:T(8,128)(2,1)S(1)} %multiply_convert_fusion.5), channel_id=1, source_target_pairs={{0,4},{4,8},{8,12},{12,16},{16,20},{20,24},{24,28},{1,5},{5,9},{9,... | collective-permute-start | bytes 786440 | tf_op jit(solution)/shard_map/ppermute | solution.py:18
  70.2 8.6 %collective-permute-start.1 = (bf16[2,1,64,1024]{3,2,0,1:T(8,128)(2,1)S(1)}, bf16[2,1,64,1024]{3,2,0,1:T(8,128)(2,1)S(1)}, u32[]{:S(2)}, u32[]{:S(2)}) collective-permute-start(bf16[2,1,64,1024]{3,2,0,1:T(8,128)(2,1)S(1)} %multiply_convert_fusion.5), channel_id=1, source_target_pairs={{4,0},{8,4},{12,8},{16,12},{20,16},{24,20},{28,24},{5,1},{9,5},{13... | collective-permute-start | bytes 786440 | tf_op jit(solution)/shard_map/ppermute | solution.py:20
  79.6 19.2 %copy-start.11 = (pred[2]{0:T(512)(128)(4,1)S(1)}, pred[2]{0:T(512)(128)(4,1)}, u32[]{:S(2)}) copy-start(pred[2]{0:T(512)(128)(4,1)} %copy-done.10) | copy-start | bytes 10
  79.8 19.3 %copy-start.9 = (pred[2]{0:T(512)(128)(4,1)S(1)}, pred[2]{0:T(512)(128)(4,1)}, u32[]{:S(2)}) copy-start(pred[2]{0:T(512)(128)(4,1)} %copy-done.8) | copy-start | bytes 10
  79.8 19.6 %copy-start.15 = (pred[2]{0:T(512)(128)(4,1)S(1)}, pred[2]{0:T(512)(128)(4,1)}, u32[]{:S(2)}) copy-start(pred[2]{0:T(512)(128)(4,1)} %copy-done.14) | copy-start | bytes 10
  80.0 19.7 %copy-start.13 = (pred[2]{0:T(512)(128)(4,1)S(1)}, pred[2]{0:T(512)(128)(4,1)}, u32[]{:S(2)}) copy-start(pred[2]{0:T(512)(128)(4,1)} %copy-done.12) | copy-start | bytes 10
  92.9 7.0 %copy-start.24 = (pred[2]{0:T(512)(128)(4,1)S(1)}, pred[2]{0:T(512)(128)(4,1)}, u32[]{:S(2)}) copy-start(pred[2]{0:T(512)(128)(4,1)} %copy-done.23) | copy-start | bytes 10
  92.9 7.3 %copy-start.22 = (pred[2]{0:T(512)(128)(4,1)S(1)}, pred[2]{0:T(512)(128)(4,1)}, u32[]{:S(2)}) copy-start(pred[2]{0:T(512)(128)(4,1)} %copy-done.21) | copy-start | bytes 10
  93.7 6.7 %copy-start.20 = (pred[2]{0:T(512)(128)(4,1)S(1)}, pred[2]{0:T(512)(128)(4,1)}, u32[]{:S(2)}) copy-start(pred[2]{0:T(512)(128)(4,1)} %copy-done.19) | copy-start | bytes 10
  117.2 13.5 %copy-start.2 = (bf16[2,1,64,1024]{3,2,0,1:T(8,128)(2,1)S(1)}, bf16[2,1,64,1024]{3,2,0,1:T(8,128)(2,1)}, u32[]{:S(2)}) copy-start(bf16[2,1,64,1024]{3,2,0,1:T(8,128)(2,1)} %copy-done.1) | copy-start | bytes 786436
  117.2 13.5 %copy-start.40 = (bf16[2,64,192]{2,1,0:T(8,128)(2,1)S(1)}, bf16[2,64,192]{2,1,0:T(8,128)(2,1)}, u32[]{:S(2)}) copy-start(bf16[2,64,192]{2,1,0:T(8,128)(2,1)} %param.11) | copy-start | bytes 147460
  118.0 8.5 %collective-permute-start.2 = (bf16[2,1,64,1024]{3,2,0,1:T(8,128)(2,1)S(1)}, bf16[2,1,64,1024]{3,2,0,1:T(8,128)(2,1)S(1)}, u32[]{:S(2)}, u32[]{:S(2)}) collective-permute-start(bf16[2,1,64,1024]{3,2,0,1:T(8,128)(2,1)S(1)} %multiply_convert_fusion.4), channel_id=1, source_target_pairs={{0,4},{4,8},{8,12},{12,16},{16,20},{20,24},{24,28},{1,5},{5,9},{9,... | collective-permute-start | bytes 786440 | tf_op jit(solution)/shard_map/ppermute | solution.py:18
  122.2 8.6 %collective-permute-start.3 = (bf16[2,1,64,1024]{3,2,0,1:T(8,128)(2,1)S(1)}, bf16[2,1,64,1024]{3,2,0,1:T(8,128)(2,1)S(1)}, u32[]{:S(2)}, u32[]{:S(2)}) collective-permute-start(bf16[2,1,64,1024]{3,2,0,1:T(8,128)(2,1)S(1)} %multiply_convert_fusion.4), channel_id=1, source_target_pairs={{4,0},{8,4},{12,8},{16,12},{20,16},{24,20},{28,24},{5,1},{9,5},{13... | collective-permute-start | bytes 786440 | tf_op jit(solution)/shard_map/ppermute | solution.py:20
  (21 other events, 63.8 us)
where the time goes:
time: 132 us
  local copies, waits for them, and re-layouts  38.7 us (29%)
  blocking collectives  35.3 us (27%)
  matrix products  17.8 us (13%)
  starting transfers between devices  16.3 us (12%)
  waiting for transfers between devices  13.3 us (10%)
  other arithmetic  8.66 us (7%)
  between operations  1.66 us (1%)
    all_gather x2, blocking collectives, shards(): lax.all_gather(strips(tiles_view, 3), 'plane', axis=0, tiled=True)  26 us
    dot_general x54, matrix products, plane_conv(): jnp.einsum('ok,nskq->nsoq', weight[:, tap * channels:(tap + 1) * channels...  16.6 us
    gather x24, local copies, waits for them, and re-layouts, fetch_strip(): strip_pool[safe_index[:, column]]  14.7 us
    ppermute x2, starting transfers between devices, with_halo(): lax.ppermute(tail, axis, [(i, (i + 1) % count) for i in range(ends)])  12.5 us
    ppermute x2, waiting for transfers between devices, with_halo(): lax.ppermute(head, axis, [((i + 1) % count, i) for i in range(ends)])  9.57 us
    all_gather x1, blocking collectives, shards(): lax.all_gather(strips(mask_tiles, 2), 'plane', axis=0, tiled=True)  9.34 us
    slice x12, local copies, waits for them, and re-layouts, plane_conv(): total[..., :span].reshape(total.shape[:-1] + (inner, side))[..., :inner]  7.78 us
    reshape x6, local copies, waits for them, and re-layouts, plane_conv(): return result.reshape(result.shape[:-2] + (inner * inner,))  5.96 us
  transfers between devices with their start and end apart: 4, of which 4 were waited for; matrix products, arithmetic and copies ran while one was open for 0% of the time, Pallas kernels for 0%

commit v1 on v0

v1 whole, which is shorter than its diff:
```python
import functools
import math

import jax
import jax.numpy as jnp
from jax import lax
from jax.experimental import pallas as pl
from jax.experimental.pallas import tpu as pltpu
from jax.sharding import PartitionSpec as P

F32 = jnp.float32
BF16 = jnp.bfloat16
LANES = 128
BLOCK = 256
FRONT = LANES
AUG = 8
LAYERS = 3


class Geometry:
    def __init__(self, cells, blocks):
        self.tile = math.isqrt(cells)
        self.halo = LAYERS * blocks
        self.side = self.tile + 2 * self.halo
        self.blocks = blocks
        body = -(-self.side * self.side // BLOCK) * BLOCK
        self.body = body
        self.width = FRONT + body + LANES
        self.strip = self.halo * self.tile

    def lane(self, row, col):
        return FRONT + row * self.side + col

    def span(self, margin):
        first = self.lane(margin, margin)
        last = self.lane(self.side - 1 - margin, self.side - 1 - margin)
        return first // LANES * LANES, (last // LANES + 1) * LANES


def whole():
    return pl.BlockSpec(memory_space=pltpu.VMEM)


def scalars():
    return pl.BlockSpec(memory_space=pltpu.SMEM)


def params(mib=20):
    return pltpu.CompilerParams(vmem_limit_bytes=mib << 20)


def cost(flops, moved=1 << 20):
    return pl.CostEstimate(flops=flops, bytes_accessed=moved, transcendentals=0)


def iota(shape, dim):
    return lax.broadcasted_iota(jnp.int32, shape, dim)


def one_hot(condition):
    return jnp.where(condition, 1.0, 0.0).astype(BF16)


def dot(a, b):
    return jnp.dot(a, b, preferred_element_type=F32)


KIND = (0, 0, 0, 2, 3, 1, 1, 1)


def pack_kernel(g, slots, planes, nbr_ref, counts_ref, acts_ref, mask_ref, *refs):
    out_refs, (aug_ref, strip_ref) = refs[:planes], refs[planes:]
    me = lax.axis_index("plane")
    tile, halo = g.tile, g.halo
    cells = tile * tile
    rows = acts_ref.shape[2]
    per_tile = LANES // tile
    half = LANES // 2
    lane = iota((cells, 2 * LANES), 1)
    lane = jnp.where(lane >= LANES + half, lane - half, lane)
    source = iota((cells, 2 * LANES), 0)
    row, col = source // tile, source % tile
    left = one_hot((row * halo + col == lane) & (col < halo))
    right = one_hot((row * halo + col - (tile - halo) == lane) & (col >= tile - halo))
    i, j = iota((LANES, LANES), 0), iota((LANES, LANES), 1)
    low = one_hot(i == j % half)
    high = one_hot(i == half + j % half)
    for a in range(slots):
        alive = a < counts_ref[me]
        aug_ref[a, :rows] = jnp.where(alive, acts_ref[a, 0].astype(F32), 0.0).astype(BF16)
        line = mask_ref[a, 0:1].astype(F32)
        aug_ref[a, rows:] = jnp.where(iota((AUG, cells), 0) == 0, line, 0.0).astype(BF16)
        x = aug_ref[a]
        strip_ref[a, 0, 0] = x[:, :LANES]
        strip_ref[a, 0, 1] = dot(x[:, LANES : 2 * LANES], low).astype(BF16)
        strip_ref[a, 1, 0] = x[:, cells - LANES :]
        strip_ref[a, 1, 1] = dot(x[:, cells - 2 * LANES : cells - LANES], high).astype(BF16)
        for kind, pick in ((2, left), (3, right)):
            both = dot(x, pick).astype(BF16)
            strip_ref[a, kind, 0] = both[:, :LANES]
            strip_ref[a, kind, 1] = both[:, LANES:]
    lower = iota((rows + AUG, LANES), 1) < half
    for k in range(planes):
        peer = partner(me, k, planes, True)
        for a in range(slots):
            kinds = []
            for b in range(slots):
                kind = jnp.int32(0)
                for d in range(8):
                    kind = jnp.where(nbr_ref[a, d] == peer * slots + b, KIND[d], kind)
                kinds.append(kind)
                out_refs[k][slots * a + b] = strip_ref[a, kind, 0]
            out_refs[k][slots * slots + a] = jnp.where(lower, strip_ref[a, kinds[0], 1], strip_ref[a, kinds[1], 1])


def partner(me, k, planes, outgoing):
    if planes & (planes - 1) == 0:
        return me ^ k
    return lax.rem(me + (k if outgoing else planes - k), planes)


def route(me, other, planes):
    if planes & (planes - 1) == 0:
        return me ^ other
    return lax.rem(me - other + planes, planes)


def halo_pieces(g):
    tile, halo, side = g.tile, g.halo, g.side
    pieces = []
    for d in (0, 1, 2, 5, 6, 7):
        first_row = 0 if d < 3 else halo + tile
        cols = {0: (0, halo), 1: (halo, halo + tile), 2: (halo + tile, side)}[d % 3 if d < 3 else (d - 5)]
        blocks = sorted({((first_row + r) * side + c) // BLOCK for r in range(halo) for c in range(*cols)})
        pieces += [(d, n) for n in blocks]
    sides = []
    split = LANES // halo
    for part in (0, 1):
        blocks = set()
        for r in range(tile):
            for c in range(halo):
                if (r * halo + c >= LANES) == bool(part):
                    blocks.add(((halo + r) * side + c) // BLOCK)
                    blocks.add(((halo + r) * side + halo + tile + c) // BLOCK)
        sides += [(part, n) for n in sorted(blocks)]
    return pieces, sides


def cell_of(e, g):
    return e // g.tile, e % g.tile


def strip_entry(lane, b, half):
    rest = lane - LANES
    ours = (rest >= b * half) & (rest < (b + 1) * half)
    return jnp.where(lane < LANES, lane, jnp.where(ours, LANES + rest - b * half, -10000))


def own_band(g):
    pairs = set()
    for r in range(g.tile):
        for c in range(g.tile):
            pairs.add(((r * g.tile + c) // BLOCK, ((r + g.halo) * g.side + c + g.halo) // BLOCK))
    return sorted(pairs)


def prepare_kernel(g, slots, nbr_ref, counts_ref, acts_ref, mask_ref, own_ref, pick_ref, keep_ref, aug_ref):
    me = lax.axis_index("plane")
    tile, halo, side = g.tile, g.halo, g.side
    cells = tile * tile
    rows = acts_ref.shape[2]
    half = LANES // 2
    for a in range(slots):
        alive = a < counts_ref[me]
        aug_ref[a, :rows] = jnp.where(alive, acts_ref[a, 0].astype(F32), 0.0).astype(BF16)
        line = mask_ref[a, 0:1].astype(F32)
        aug_ref[a, rows:] = jnp.where(iota((AUG, cells), 0) == 0, line, 0.0).astype(BF16)
    src = iota((BLOCK, BLOCK), 0)
    dst = iota((BLOCK, BLOCK), 1)
    pairs = own_band(g)
    for n in range(g.body // BLOCK):
        total = [jnp.zeros((rows + AUG, BLOCK), F32) for _ in range(slots)]
        for k in [k for k, m in pairs if m == n]:
            cell = src + k * BLOCK
            where = (cell // tile + halo) * side + cell % tile + halo
            move = one_hot(where == dst + n * BLOCK)
            for a in range(slots):
                total[a] += dot(aug_ref[a, :, k * BLOCK : (k + 1) * BLOCK], move)
        for a in range(slots):
            own_ref[a, :, n * BLOCK : (n + 1) * BLOCK] = total[a].astype(BF16)
    pieces, sides = halo_pieces(g)
    at = 0
    for d, n in pieces:
        for b in range(slots):
            e = strip_entry(src, b, half)
            if d < 3:
                lead = g.strip - LANES
                e = jnp.where(src < LANES, src + lead, e - LANES)
                row, col, base = e // tile, e % tile, 0
            else:
                row, col, base = e // tile, e % tile, halo + tile
            kind = d if d < 3 else d - 5
            if kind == 0:
                good, shift = col >= tile - halo, halo - tile
            elif kind == 1:
                good, shift = col >= 0, halo
            else:
                good, shift = col < halo, halo + tile
            where = (base + row) * side + col + shift
            pick_ref[at] = one_hot((where == dst + n * BLOCK) & good & (e >= 0))
            at += 1
    for part, n in sides:
        for b in range(slots):
            lane = jnp.where(src < LANES, src, src - LANES) + part * LANES
            e = strip_entry(lane, b, half)
            row, col = e // halo, e % halo
            where = (halo + row) * side + col + jnp.where(src < LANES, 0, halo + tile)
            pick_ref[at] = one_hot((where == dst + n * BLOCK) & (e >= 0))
            at += 1
    start, _ = g.span(halo)
    for m, (n, k) in enumerate(keep_band(g)):
        cell = dst + n * BLOCK
        where = FRONT + (cell // tile + halo) * side + cell % tile + halo - start
        keep_ref[m] = one_hot(where == src + k * BLOCK)


def keep_band(g):
    start, _ = g.span(g.halo)
    pairs = set()
    for r in range(g.tile):
        for c in range(g.tile):
            pairs.add(((r * g.tile + c) // BLOCK, (g.lane(r + g.halo, c + g.halo) - start) // BLOCK))
    return sorted(pairs)


def conv(g, x_ref, y_ref, stack_ref, weight, bias, mask_ref, start, stop):
    channels = weight.shape[0]
    width = stop - start
    for row in range(3):
        for col in range(3):
            tap = row * 3 + col
            off = start + (row - 1) * g.side + col - 1
            stack_ref[tap * channels : (tap + 1) * channels, :width] = x_ref[:, off : off + width]
    for at in range(0, width, BLOCK):
        size = min(BLOCK, width - at)
        total = dot(weight, stack_ref[:, at : at + size])
        half = 0.5 * (total + bias)
        out = (half + half * jnp.tanh(half)) * mask_ref[0:1, start + at : start + at + size]
        y_ref[:, start + at : start + at + size] = out.astype(BF16)


def branch(g, block, bufs, stack_ref, weight_ref, bias_ref, mask_ref):
    margin = LAYERS * block + 1
    for layer in range(LAYERS):
        start, stop = g.span(margin + layer)
        conv(
            g,
            bufs[layer % 2],
            bufs[(layer + 1) % 2],
            stack_ref,
            weight_ref[block, layer],
            bias_ref[block, layer],
            mask_ref,
            start,
            stop,
        )
    return bufs[LAYERS % 2]


def first_kernel(g, slots, planes, nbr_ref, own_ref, pick_ref, weight_ref, bias_ref, *refs):
    messages = refs[:planes]
    branch_ref, hidden_ref, mask_ref, pool_ref, x_ref, y_ref, stack_ref = refs[planes:]
    me = lax.axis_index("plane")
    channels = weight_ref.shape[2]
    for k in range(planes):
        pool_ref[k] = messages[k][...]
    pieces, sides = halo_pieces(g)
    start, stop = g.span(LAYERS)
    for b in range(slots):

        def fetch(d):
            source = nbr_ref[b, d]
            safe = jnp.maximum(source, 0)
            k = route(me, safe // slots, planes)
            a = safe % slots
            ok = source >= 0
            main = pool_ref[k, slots * a + b]
            rest = pool_ref[k, slots * slots + a]
            main = jnp.where(ok, main.astype(F32), 0.0).astype(BF16)
            rest = jnp.where(ok, rest.astype(F32), 0.0).astype(BF16)
            return main, rest

        strips = {d: fetch(d) for d in range(8)}
        lines = {d: jnp.concatenate(strips[d], axis=1) for d in (0, 1, 2, 5, 6, 7)}
        walls = [jnp.concatenate([strips[3][part], strips[4][part]], axis=1) for part in (0, 1)]
        for n in range(g.body // BLOCK):
            total = own_ref[b, :, n * BLOCK : (n + 1) * BLOCK].astype(F32)
            for at, (d, m) in enumerate(pieces):
                if m == n:
                    total += dot(lines[d], pick_ref[at * slots + b])
            for at, (part, m) in enumerate(sides):
                if m == n:
                    total += dot(walls[part], pick_ref[(len(pieces) + at) * slots + b])
            lanes = slice(FRONT + n * BLOCK, FRONT + (n + 1) * BLOCK)
            x_ref[b, :, lanes] = total[:channels].astype(BF16)
            mask_ref[b, :, lanes] = total[channels:]
        x_ref[b, :, :FRONT] = jnp.zeros((channels, FRONT), BF16)
        x_ref[b, :, FRONT + g.body :] = jnp.zeros((channels, LANES), BF16)
        y_ref[b] = jnp.zeros(y_ref.shape[1:], BF16)
        hidden_ref[b] = x_ref[b, :, start:stop]
        out = branch(g, 0, (x_ref.at[b], y_ref.at[b]), stack_ref.at[b], weight_ref, bias_ref, mask_ref.at[b])
        branch_ref[b] = out[:, start:stop]


def depth_sum(block, bias_ref, weight_ref, pair_tap, other_tap, own, pair, other):
    total = dot(weight_ref[block, 1], own)
    total += dot(weight_ref[block, pair_tap], pair)
    total += dot(weight_ref[block, other_tap], other)
    return total + bias_ref[block]


def depth_taps():
    odd = lax.rem(lax.axis_index("depth"), 2)
    return 2 - 2 * odd, 2 * odd


def second_kernel(
    g,
    slots,
    own_ref,
    pair_ref,
    other_ref,
    hidden_ref,
    mask_ref,
    keep_ref,
    weight_ref,
    bias_ref,
    dweight_ref,
    dbias_ref,
    branch_ref,
    kept_ref,
    x_ref,
    y_ref,
    stack_ref,
):
    pair_tap, other_tap = depth_taps()
    start, stop = g.span(LAYERS)
    inner, outer = g.span(g.halo)
    band = keep_band(g)
    cells = g.tile * g.tile

    def keep(buf, ref):
        for n in range(cells // BLOCK):
            total = None
            for m, (i, k) in enumerate(band):
                if i == n:
                    lo = inner + k * BLOCK
                    term = dot(buf[:, lo : lo + BLOCK], keep_ref[m])
                    total = term if total is None else total + term
            ref[:, n * BLOCK : (n + 1) * BLOCK] = total.astype(BF16)

    for b in range(slots):
        x_ref[b, :, :start] = jnp.zeros((x_ref.shape[1], start), BF16)
        x_ref[b, :, stop:] = jnp.zeros((x_ref.shape[1], x_ref.shape[2] - stop), BF16)
        y_ref[b] = jnp.zeros(y_ref.shape[1:], BF16)
        for at in range(0, stop - start, BLOCK):
            size = min(BLOCK, stop - start - at)
            piece = slice(at, at + size)
            summed = depth_sum(
                0, dbias_ref, dweight_ref, pair_tap, other_tap, own_ref[b, :, piece], pair_ref[b, :, piece], other_ref[b, :, piece]
            )
            lanes = slice(start + at, start + at + size)
            x_ref[b, :, lanes] = (hidden_ref[b, :, piece].astype(F32) + mask_ref[b, 0:1, lanes] * summed).astype(BF16)
        keep(x_ref.at[b], kept_ref.at[b])
        out = branch(g, 1, (x_ref.at[b], y_ref.at[b]), stack_ref.at[b], weight_ref, bias_ref, mask_ref.at[b])
        keep(out, branch_ref.at[b])


def last_kernel(slots, block, own_ref, pair_ref, other_ref, kept_ref, mask_ref, dweight_ref, dbias_ref, out_ref):
    pair_tap, other_tap = depth_taps()
    for b in range(slots):
        summed = depth_sum(block, dbias_ref, dweight_ref, pair_tap, other_tap, own_ref[b], pair_ref[b], other_ref[b])
        mask = mask_ref[b, 0:1].astype(F32)
        out_ref[b, 0] = (kept_ref[b].astype(F32) + mask * summed).astype(BF16)


def neighbours_in_depth(x):
    count = lax.axis_size("depth")

    def swap(first):
        perm = []
        for i in range(first, count - 1, 2):
            perm += [(i, i + 1), (i + 1, i)]
        return lax.ppermute(x, "depth", perm)

    other = swap(1)
    pair = swap(0)
    return pair, other


def shards(
    activations, plane_weight, plane_bias, depth_weight, depth_bias, counts, neighbours, voxel_mask
):
    slots, sections, channels, cells = activations.shape
    blocks = plane_weight.shape[0]
    planes = lax.axis_size("plane")
    assert slots == 2 and sections == 1 and blocks == 2
    g = Geometry(cells, blocks)
    bias = plane_bias[..., None]
    dbias = depth_bias[..., None]
    dweight = depth_weight.reshape(blocks, channels, 3, channels).transpose(0, 2, 1, 3)
    rows = channels + AUG
    message = jax.ShapeDtypeStruct((slots * slots + slots, rows, LANES), BF16)
    packed = pl.pallas_call(
        functools.partial(pack_kernel, g, slots, planes),
        out_shape=[message] * planes,
        in_specs=[scalars(), scalars(), whole(), whole()],
        out_specs=[whole()] * planes,
        scratch_shapes=[
            pltpu.VMEM((slots, rows, cells), BF16),
            pltpu.VMEM((slots, 4, 2, rows, LANES), BF16),
        ],
        compiler_params=params(),
        cost_estimate=cost(1 << 28),
        name="pack",
    )(neighbours, counts, activations, voxel_mask)
    received = [packed[0]] + [None] * (planes - 1)
    for k in reversed(range(1, planes)):
        if planes & (planes - 1) == 0:
            perm = [(i, i ^ k) for i in range(planes)]
        else:
            perm = [(i, (i + k) % planes) for i in range(planes)]
        received[k] = lax.ppermute(packed[k], "plane", perm)

    pieces, sides = halo_pieces(g)
    own, pick, keep = pl.pallas_call(
        functools.partial(prepare_kernel, g, slots),
        out_shape=[
            jax.ShapeDtypeStruct((slots, rows, g.body), BF16),
            jax.ShapeDtypeStruct(((len(pieces) + len(sides)) * slots, BLOCK, BLOCK), BF16),
            jax.ShapeDtypeStruct((len(keep_band(g)), BLOCK, BLOCK), BF16),
        ],
        in_specs=[scalars(), scalars(), whole(), whole()],
        out_specs=[whole()] * 3,
        scratch_shapes=[pltpu.VMEM((slots, rows, cells), BF16)],
        compiler_params=params(),
        cost_estimate=cost(1 << 29),
        name="prepare",
    )(neighbours, counts, activations, voxel_mask)

    start, stop = g.span(LAYERS)
    work = [
        pltpu.VMEM((slots, channels, g.width), BF16),
        pltpu.VMEM((slots, channels, g.width), BF16),
        pltpu.VMEM((slots, 9 * channels, g.body), BF16),
    ]
    wide = jax.ShapeDtypeStruct((slots, channels, stop - start), BF16)
    branch0, hidden0, mask = pl.pallas_call(
        functools.partial(first_kernel, g, slots, planes),
        out_shape=[wide, wide, jax.ShapeDtypeStruct((slots, AUG, g.width), F32)],
        in_specs=[scalars()] + [whole()] * (4 + planes),
        out_specs=[whole()] * 3,
        scratch_shapes=[pltpu.VMEM((planes,) + message.shape, BF16)] + work,
        compiler_params=params(30),
        cost_estimate=cost(1 << 31),
        name="first",
    )(neighbours, own, pick, plane_weight, bias, *received)
    pair, other = neighbours_in_depth(branch0)
    narrow = jax.ShapeDtypeStruct((slots, channels, cells), BF16)
    branch1, kept = pl.pallas_call(
        functools.partial(second_kernel, g, slots),
        out_shape=[narrow, narrow],
        in_specs=[whole()] * 10,
        out_specs=[whole()] * 2,
        scratch_shapes=work,
        compiler_params=params(30),
        cost_estimate=cost(1 << 31),
        name="second",
    )(branch0, pair, other, hidden0, mask, keep, plane_weight, bias, dweight, dbias)
    pair, other = neighbours_in_depth(branch1)
    return pl.pallas_call(
        functools.partial(last_kernel, slots, blocks - 1),
        out_shape=jax.ShapeDtypeStruct(activations.shape, BF16),
        in_specs=[whole()] * 7,
        out_specs=whole(),
        compiler_params=params(),
        cost_estimate=cost(1 << 26),
        name="last",
    )(branch1, pair, other, kept, voxel_mask, dweight, dbias)


def solution(mesh):
    in_specs = (
        P("plane", "depth", None, None),
        P(),
        P(),
        P(),
        P(),
        P(),
        P("plane", None),
        P("plane", "depth", None),
    )
    out_specs = P("plane", "depth", None, None)
    return jax.shard_map(shards, mesh=mesh, in_specs=in_specs, out_specs=out_specs, check_vma=False)
```

time: 132 us -> 62.7 us (0.48)
  blocking collectives: 35.3 us -> 0 us
  local copies, waits for them, and re-layouts: 38.7 us -> 13 us
  matrix products: 17.8 us -> 0 us
  Pallas kernels: 0 us -> 16.5 us
  other arithmetic: 8.66 us -> 0 us
  waiting for transfers between devices: 13.3 us -> 18.8 us
  starting transfers between devices: 16.3 us -> 13.1 us
  between operations: 1.66 us -> 0.15 us
    all_gather x3 -> x0, blocking collectives: 35.3 us -> none  [the longest x2 26 us: shards(): lax.all_gather(strips(tiles_view, 3), 'plane', axis=0, tiled=True)]
    dot_general x56 -> x0, matrix products: 17.8 us -> none  [the longest x54 16.6 us: plane_conv(): jnp.einsum('ok,nskq->nsoq', weight[:, tap * channels:(tap + 1) * channels...]
    pallas_call x0 -> x5, Pallas kernels: none -> 16.5 us  [the longest x1 7.1 us: shards(): pl.pallas_call(functools.partial(first_kernel, g, slots, planes), out_sha...]
    gather x24 -> x0, local copies, waits for them, and re-layouts: 14.7 us -> none  [fetch_strip(): strip_pool[safe_index[:, column]]]
    slice x65 -> x0, local copies, waits for them, and re-layouts: 12.8 us -> none  [the longest x12 7.78 us: plane_conv(): total[..., :span].reshape(total.shape[:-1] + (inner, side))[..., :inner]]
    unnamed x84 -> x35, local copies, waits for them, and re-layouts: 0.88 us -> 12 us
    reshape x29 -> x1, local copies, waits for them, and re-layouts: 8.52 us -> 0.13 us  [shards(): depth_weight.reshape(blocks, channels, 3, channels).transpose(0, 2, 1, 3)]
    ppermute x4 -> x7, waiting for transfers between devices: 13.3 us -> 18.8 us  [the longest x4 17.4 us: swap(): return lax.ppermute(x, 'depth', perm)]
  transfers between devices with their start and end apart: 4 -> 7, of which waited for: 4 -> 3; matrix products, arithmetic and copies ran while one was open for 0% -> 3% of each run, Pallas kernels for 0% -> 3%
where the time goes in v1:
time: 62.7 us; the launch traced here: 61.6 us
  waiting for transfers between devices  18.8 us (30%)
  Pallas kernels  16.5 us (26%)
  starting transfers between devices  13.1 us (21%)
  local copies, waits for them, and re-layouts  13 us (21%)
    ppermute x4, waiting for transfers between devices, swap(): return lax.ppermute(x, 'depth', perm)  17.4 us
    unnamed x35, local copies, waits for them, and re-layouts  12 us
    ppermute x4, starting transfers between devices, swap(): return lax.ppermute(x, 'depth', perm)  9.45 us
    pallas_call x1, Pallas kernels, shards(): pl.pallas_call(functools.partial(first_kernel, g, slots, planes), out_sha...  7.1 us
    pallas_call x1, Pallas kernels, shards(): pl.pallas_call(functools.partial(second_kernel, g, slots), out_shape=[nar...  5.3 us
    ppermute x3, starting transfers between devices, shards(): received[k] = lax.ppermute(packed[k], 'plane', perm)  3.67 us
    pallas_call x1, Pallas kernels, shards(): pl.pallas_call(functools.partial(prepare_kernel, g, slots), out_shape=[ja...  1.92 us
    ppermute x3, waiting for transfers between devices, shards(): received[k] = lax.ppermute(packed[k], 'plane', perm)  1.4 us
  transfers between devices with their start and end apart: 7, of which 3 were waited for; matrix products, arithmetic and copies ran while one was open for 3% of the time, Pallas kernels for 3%

profile of v1, /device:TPU:3, one launch (start us, length us, event | category | flops | bytes accessed | tf_op | source)
XLA Modules:
  0.0 61.6 jit_solution(4201291540139641937)
XLA Ops:
  0.0 0.7 %copy-done = s32[2,1,1024]{2,1,0:T(1,128)S(1)} copy-done((s32[2,1,1024]{2,1,0:T(1,128)S(1)}, s32[2,1,1024]{2,1,0:T(1,128)}, u32[]{:S(2)}) %copy-start) | copy-done | bytes 8216
  0.7 0.9 %copy-done.5 = bf16[2,1,64,1024]{3,2,1,0:T(8,128)(2,1)S(1)} copy-done((bf16[2,1,64,1024]{3,2,1,0:T(8,128)(2,1)S(1)}, bf16[2,1,64,1024]{3,2,1,0:T(8,128)(2,1)}, u32[]{:S(2)}) %copy-start.5) | copy-done | bytes 262168
  1.7 0.7 %copy-done.7 = s32[2,8]{1,0:T(2,128)S(1)} copy-done((s32[2,8]{1,0:T(2,128)S(1)}, s32[2,8]{1,0:T(2,128)}, u32[]{:S(2)}) %copy-start.7) | copy-done | bytes 88
  3.0 1.2 %pack.1 = (bf16[6,72,128]{2,1,0:T(8,128)(2,1)S(1)}, bf16[6,72,128]{2,1,0:T(8,128)(2,1)S(1)}, bf16[6,72,128]{2,1,0:T(8,128)(2,1)S(1)}, bf16[6,72,128]{2,1,0:T(8,128)(2,1)S(1)}) custom-call(s32[2,8]{1,0:T(2,128)S(1)} %copy-done.7, s32[4]{0:T(128)S(1)} %copy-done.10, bf16[2,1,64,1024]{3,2,1,0:T(8,128)(2,1)S(1)} %copy-done.5, s32[2,1,1024]{2,1,0:T(1,128)S(1)} %copy-done), custom_call_target="tpu_custom_call" | custom-call | flops 268435456 | bytes 1048576 | tf_op jit(solution)/shard_map/pack/pallas_call | solution.py:414
  4.1 1.4 %collective-permute-start = (bf16[6,72,128]{2,1,0:T(8,128)(2,1)S(1)}, bf16[6,72,128]{2,1,0:T(8,128)(2,1)S(1)}, u32[]{:S(2)}, u32[]{:S(2)}) collective-permute-start(bf16[6,72,128]{2,1,0:T(8,128)(2,1)S(1)} %get-tuple-element.20), channel_id=1, source_target_pairs={{0,1},{1,0},{2,3},{3,2},{4,5},{5,4},{6,7},{7,6},{8,9},{9,8},{10,11... | collective-permute-start | bytes 331784 | tf_op jit(solution)/shard_map/ppermute | solution.py:433
  5.5 2.3 %collective-permute-start.1 = (bf16[6,72,128]{2,1,0:T(8,128)(2,1)S(1)}, bf16[6,72,128]{2,1,0:T(8,128)(2,1)S(1)}, u32[]{:S(2)}, u32[]{:S(2)}) collective-permute-start(bf16[6,72,128]{2,1,0:T(8,128)(2,1)S(1)} %get-tuple-element.21), channel_id=1, source_target_pairs={{0,2},{1,3},{2,0},{3,1},{4,6},{5,7},{6,4},{7,5},{8,10},{9,11},{10,... | collective-permute-start | bytes 331784 | tf_op jit(solution)/shard_map/ppermute | solution.py:433
  7.8 0.8 %copy.12.bias_ref = f32[2,3,64,1]{3,2,1,0:T(8,128)S(1)} copy(f32[2,3,64,1]{2,0,1,3:T(2,128)} %bitcast.7) | data formatting | bytes 3072 | tf_op jit(solution)/shard_map/broadcast_in_dim | solution.py:409
  8.6 0.7 %copy-done.1 = s32[2,1,1024]{2,1,0:T(1,128)S(1)} copy-done((s32[2,1,1024]{2,1,0:T(1,128)S(1)}, s32[2,1,1024]{2,1,0:T(1,128)}, u32[]{:S(2)}) %copy-start.1) | copy-done | bytes 8216
  9.3 0.9 %copy-done.6 = bf16[2,1,64,1024]{3,2,1,0:T(8,128)(2,1)S(1)} copy-done((bf16[2,1,64,1024]{3,2,1,0:T(8,128)(2,1)S(1)}, bf16[2,1,64,1024]{3,2,1,0:T(8,128)(2,1)}, u32[]{:S(2)}) %copy-start.6) | copy-done | bytes 262168
  11.6 1.9 %prepare.1 = (bf16[2,72,2048]{2,1,0:T(8,128)(2,1)S(1)}, bf16[36,256,256]{2,1,0:T(8,128)(2,1)S(1)}, bf16[9,256,256]{2,1,0:T(8,128)(2,1)S(1)}) custom-call(s32[2,8]{1,0:T(2,128)S(1)} %copy-done.8, s32[4]{0:T(128)S(1)} %copy-done.11, bf16[2,1,64,1024]{3,2,1,0:T(8,128)(2,1)S(1)} %copy-done.6, s32[2,1,1024]{2,1,0:T(1,128)S(1)} %copy-done.1), custom_call_target="tpu_custom_call" | custom-call | flops 536870912 | bytes 1048576 | tf_op jit(solution)/shard_map/prepare/pallas_call | solution.py:436
  13.6 1.4 %collective-permute-done.2.refs_3_ = bf16[6,72,128]{2,1,0:T(8,128)(2,1)S(1)} collective-permute-done((bf16[6,72,128]{2,1,0:T(8,128)(2,1)S(1)}, bf16[6,72,128]{2,1,0:T(8,128)(2,1)S(1)}, u32[]{:S(2)}, u32[]{:S(2)}) %collective-permute-start.2) | collective-permute-done | bytes 110624 | tf_op jit(solution)/shard_map/ppermute | solution.py:433
  15.0 1.0 %copy-done.3 = bf16[2,3,64,576]{3,2,1,0:T(8,128)(2,1)S(1)} copy-done((bf16[2,3,64,576]{3,2,1,0:T(8,128)(2,1)S(1)}, bf16[2,3,64,576]{3,2,1,0:T(8,128)(2,1)}, u32[]{:S(2)}) %copy-start.3) | copy-done | bytes 442392
  16.7 7.1 %first.1 = (bf16[2,64,1792]{2,1,0:T(8,128)(2,1)S(1)}, bf16[2,64,1792]{2,1,0:T(8,128)(2,1)S(1)}, f32[2,8,2304]{2,1,0:T(8,128)S(1)}) custom-call(s32[2,8]{1,0:T(2,128)S(1)} %copy-done.9, bf16[2,72,2048]{2,1,0:T(8,128)(2,1)S(1)} %get-tuple-element.17.own_ref, bf16[36,256,256]{2,1,0:T(8,128)(2,1)S(1)} %get-tuple-element.18.pick_ref, ...), custom_call_target="tpu_custom_call" | custom-call | flops 2147483648 | bytes 1048576 | tf_op jit(solution)/shard_map/first/pallas_call | solution.py:458
  23.8 0.8 %copy-done.12 = bf16[2,64,1792]{2,1,0:T(8,128)(2,1)} copy-done((bf16[2,64,1792]{2,1,0:T(8,128)(2,1)}, bf16[2,64,1792]{2,1,0:T(8,128)(2,1)S(1)}, u32[]{:S(2)}) %copy-start.12) | copy-done | bytes 458776
  25.2 2.9 %collective-permute-start.3 = (bf16[2,64,1792]{2,1,0:T(8,128)(2,1)S(1)}, bf16[2,64,1792]{2,1,0:T(8,128)(2,1)S(1)}, u32[]{:S(2)}, u32[]{:S(2)}) collective-permute-start(bf16[2,64,1792]{2,1,0:T(8,128)(2,1)S(1)} %get-tuple-element.23.own_ref), channel_id=1, source_target_pairs={{0,4},{4,0},{8,12},{12,8},{16,20},{20,16},{24,28},{28,24},{1,5},{5... | collective-permute-start | bytes 1376264 | tf_op jit(solution)/shard_map/ppermute | solution.py:394
  28.1 3.3 %collective-permute-start.4 = (bf16[2,64,1792]{2,1,0:T(8,128)(2,1)S(1)}, bf16[2,64,1792]{2,1,0:T(8,128)(2,1)S(1)}, u32[]{:S(2)}, u32[]{:S(2)}) collective-permute-start(bf16[2,64,1792]{2,1,0:T(8,128)(2,1)S(1)} %get-tuple-element.23.own_ref), channel_id=1, source_target_pairs={{4,8},{8,4},{12,16},{16,12},{20,24},{24,20},{5,9},{9,5},{13,17},{1... | collective-permute-start | bytes 1376264 | tf_op jit(solution)/shard_map/ppermute | solution.py:394
  31.4 1.0 %copy.13 = bf16[2,64,192]{1,2,0:T(8,128)(2,1)S(1)} copy(bf16[2,64,192]{2,1,0:T(8,128)(2,1)} %param.11) | data formatting | bytes 98304 | tf_op args[3]
  32.7 10.6 %collective-permute-done.4.other_ref = bf16[2,64,1792]{2,1,0:T(8,128)(2,1)S(1)} collective-permute-done((bf16[2,64,1792]{2,1,0:T(8,128)(2,1)S(1)}, bf16[2,64,1792]{2,1,0:T(8,128)(2,1)S(1)}, u32[]{:S(2)}, u32[]{:S(2)}) %collective-permute-start.4) | collective-permute-done | bytes 458784 | tf_op jit(solution)/shard_map/ppermute | solution.py:394
  43.2 1.0 %copy-done.13 = bf16[2,64,1792]{2,1,0:T(8,128)(2,1)S(1)} copy-done((bf16[2,64,1792]{2,1,0:T(8,128)(2,1)S(1)}, bf16[2,64,1792]{2,1,0:T(8,128)(2,1)}, u32[]{:S(2)}) %copy-start.13) | copy-done | bytes 458776
  44.2 0.9 %copy-done.15 = f32[2,8,2304]{2,1,0:T(8,128)S(1)} copy-done((f32[2,8,2304]{2,1,0:T(8,128)S(1)}, f32[2,8,2304]{2,1,0:T(8,128)}, u32[]{:S(2)}) %copy-start.15) | copy-done | bytes 147480
  45.2 5.3 %second.1 = (bf16[2,64,1024]{2,1,0:T(8,128)(2,1)S(1)}, bf16[2,64,1024]{2,1,0:T(8,128)(2,1)S(1)}) custom-call(bf16[2,64,1792]{2,1,0:T(8,128)(2,1)S(1)} %get-tuple-element.23.own_ref, bf16[2,64,1792]{2,1,0:T(8,128)(2,1)S(1)} %collective-permute-done.3.pair_ref, bf16[2,64,1792]{2,1,0:T(8,128)(2,1)S(1)} %collective-permute-done.4.other_ref, ...), custom_call_target="tpu_custom_call" | custom-call | flops 2147483648 | bytes 1048576 | tf_op jit(solution)/shard_map/second/pallas_call | solution.py:470
  50.5 3.2 %collective-permute-start.6 = (bf16[2,64,1024]{2,1,0:T(8,128)(2,1)S(1)}, bf16[2,64,1024]{2,1,0:T(8,128)(2,1)S(1)}, u32[]{:S(2)}, u32[]{:S(2)}) collective-permute-start(bf16[2,64,1024]{2,1,0:T(8,128)(2,1)S(1)} %get-tuple-element.27.own_ref), channel_id=1, source_target_pairs={{4,8},{8,4},{12,16},{16,12},{20,24},{24,20},{5,9},{9,5},{13,17},{1... | collective-permute-start | bytes 786440 | tf_op jit(solution)/shard_map/ppermute | solution.py:394
  53.7 6.8 %collective-permute-done.6.other_ref = bf16[2,64,1024]{2,1,0:T(8,128)(2,1)S(1)} collective-permute-done((bf16[2,64,1024]{2,1,0:T(8,128)(2,1)S(1)}, bf16[2,64,1024]{2,1,0:T(8,128)(2,1)S(1)}, u32[]{:S(2)}, u32[]{:S(2)}) %collective-permute-start.6) | collective-permute-done | bytes 262176 | tf_op jit(solution)/shard_map/ppermute | solution.py:394
  60.6 1.1 %last.1 = bf16[2,1,64,1024]{3,2,1,0:T(8,128)(2,1)} custom-call(bf16[2,64,1024]{2,1,0:T(8,128)(2,1)S(1)} %get-tuple-element.27.own_ref, bf16[2,64,1024]{2,1,0:T(8,128)(2,1)S(1)} %collective-permute-done.5.pair_ref, bf16[2,64,1024]{2,1,0:T(8,128)(2,1)S(1)} %collective-permute-done.6.other_ref, bf16[2,64,1024]{2,1,0:T(8,128)(2,1)S(1)} %get-tuple-element.28.kept_ref, ...), custom_call_target="tpu_custom_call" | custom-call | flops 67108864 | bytes 1048576 | tf_op jit(solution)/shard_map/last/pallas_call | solution.py:481
  (33 shorter events, 3.7 us)
Async XLA Ops:
  0.0 0.7 %copy-start = (s32[2,1,1024]{2,1,0:T(1,128)S(1)}, s32[2,1,1024]{2,1,0:T(1,128)}, u32[]{:S(2)}) copy-start(s32[2,1,1024]{2,1,0:T(1,128)} %mask_ref.5) | copy-start | bytes 24580
  0.7 0.9 %copy-start.5 = (bf16[2,1,64,1024]{3,2,1,0:T(8,128)(2,1)S(1)}, bf16[2,1,64,1024]{3,2,1,0:T(8,128)(2,1)}, u32[]{:S(2)}) copy-start(bf16[2,1,64,1024]{3,2,1,0:T(8,128)(2,1)} %acts_ref.3) | copy-start | bytes 786436
  1.6 0.7 %copy-start.7 = (s32[2,8]{1,0:T(2,128)S(1)}, s32[2,8]{1,0:T(2,128)}, u32[]{:S(2)}) copy-start(s32[2,8]{1,0:T(2,128)} %nbr_ref.5) | copy-start | bytes 196
  2.3 0.7 %copy-start.10 = (s32[4]{0:T(128)S(1)}, s32[4]{0:T(128)}, u32[]{:S(2)}) copy-start(s32[4]{0:T(128)} %counts_ref.3) | copy-start | bytes 52
  4.1 9.4 %collective-permute-start = (bf16[6,72,128]{2,1,0:T(8,128)(2,1)S(1)}, bf16[6,72,128]{2,1,0:T(8,128)(2,1)S(1)}, u32[]{:S(2)}, u32[]{:S(2)}) collective-permute-start(bf16[6,72,128]{2,1,0:T(8,128)(2,1)S(1)} %get-tuple-element.20), channel_id=1, source_target_pairs={{0,1},{1,0},{2,3},{3,2},{4,5},{5,4},{6,7},{7,6},{8,9},{9,8},{10,11... | collective-permute-start | bytes 331784 | tf_op jit(solution)/shard_map/ppermute | solution.py:433
  5.5 8.1 %collective-permute-start.1 = (bf16[6,72,128]{2,1,0:T(8,128)(2,1)S(1)}, bf16[6,72,128]{2,1,0:T(8,128)(2,1)S(1)}, u32[]{:S(2)}, u32[]{:S(2)}) collective-permute-start(bf16[6,72,128]{2,1,0:T(8,128)(2,1)S(1)} %get-tuple-element.21), channel_id=1, source_target_pairs={{0,2},{1,3},{2,0},{3,1},{4,6},{5,7},{6,4},{7,5},{8,10},{9,11},{10,... | collective-permute-start | bytes 331784 | tf_op jit(solution)/shard_map/ppermute | solution.py:433
  7.8 7.1 %collective-permute-start.2 = (bf16[6,72,128]{2,1,0:T(8,128)(2,1)S(1)}, bf16[6,72,128]{2,1,0:T(8,128)(2,1)S(1)}, u32[]{:S(2)}, u32[]{:S(2)}) collective-permute-start(bf16[6,72,128]{2,1,0:T(8,128)(2,1)S(1)} %get-tuple-element.22), channel_id=1, source_target_pairs={{0,3},{1,2},{2,1},{3,0},{4,7},{5,6},{6,5},{7,4},{8,11},{9,10},{10,... | collective-permute-start | bytes 331784 | tf_op jit(solution)/shard_map/ppermute | solution.py:433
  8.6 0.7 %copy-start.1 = (s32[2,1,1024]{2,1,0:T(1,128)S(1)}, s32[2,1,1024]{2,1,0:T(1,128)}, u32[]{:S(2)}) copy-start(s32[2,1,1024]{2,1,0:T(1,128)} %mask_ref.5) | copy-start | bytes 24580
  9.3 0.9 %copy-start.6 = (bf16[2,1,64,1024]{3,2,1,0:T(8,128)(2,1)S(1)}, bf16[2,1,64,1024]{3,2,1,0:T(8,128)(2,1)}, u32[]{:S(2)}) copy-start(bf16[2,1,64,1024]{3,2,1,0:T(8,128)(2,1)} %acts_ref.3) | copy-start | bytes 786436
  10.3 0.7 %copy-start.8 = (s32[2,8]{1,0:T(2,128)S(1)}, s32[2,8]{1,0:T(2,128)}, u32[]{:S(2)}) copy-start(s32[2,8]{1,0:T(2,128)} %nbr_ref.5) | copy-start | bytes 196
  11.0 0.7 %copy-start.11 = (s32[4]{0:T(128)S(1)}, s32[4]{0:T(128)}, u32[]{:S(2)}) copy-start(s32[4]{0:T(128)} %counts_ref.3) | copy-start | bytes 52
  11.6 20.9 %copy-start.16 = (f32[2,64]{1,0:T(2,128)S(1)}, f32[2,64]{1,0:T(2,128)}, u32[]{:S(2)}) copy-start(f32[2,64]{1,0:T(2,128)} %param.12) | copy-start | bytes 1540
  11.6 31.6 %copy-start.4 = (bf16[2,3,64,576]{3,2,1,0:T(8,128)(2,1)S(1)}, bf16[2,3,64,576]{3,2,1,0:T(8,128)(2,1)}, u32[]{:S(2)}) copy-start(bf16[2,3,64,576]{3,2,1,0:T(8,128)(2,1)} %weight_ref.3) | copy-start | bytes 1327108
  15.0 1.0 %copy-start.3 = (bf16[2,3,64,576]{3,2,1,0:T(8,128)(2,1)S(1)}, bf16[2,3,64,576]{3,2,1,0:T(8,128)(2,1)}, u32[]{:S(2)}) copy-start(bf16[2,3,64,576]{3,2,1,0:T(8,128)(2,1)} %weight_ref.3) | copy-start | bytes 1327108
  16.0 0.7 %copy-start.9 = (s32[2,8]{1,0:T(2,128)S(1)}, s32[2,8]{1,0:T(2,128)}, u32[]{:S(2)}) copy-start(s32[2,8]{1,0:T(2,128)} %nbr_ref.5) | copy-start | bytes 196
  23.8 0.8 %copy-start.12 = (bf16[2,64,1792]{2,1,0:T(8,128)(2,1)}, bf16[2,64,1792]{2,1,0:T(8,128)(2,1)S(1)}, u32[]{:S(2)}) copy-start(bf16[2,64,1792]{2,1,0:T(8,128)(2,1)S(1)} %get-tuple-element.24.hidden_ref) | copy-start | bytes 1376260
  24.6 0.7 %copy-start.14 = (f32[2,8,2304]{2,1,0:T(8,128)}, f32[2,8,2304]{2,1,0:T(8,128)S(1)}, u32[]{:S(2)}) copy-start(f32[2,8,2304]{2,1,0:T(8,128)S(1)} %get-tuple-element.25.mask_ref) | copy-start | bytes 442372
  25.2 35.3 %copy-start.2 = (s32[2,1,1024]{2,1,0:T(1,128)S(1)}, s32[2,1,1024]{2,1,0:T(1,128)}, u32[]{:S(2)}) copy-start(s32[2,1,1024]{2,1,0:T(1,128)} %mask_ref.5) | copy-start | bytes 24580
  25.2 7.4 %collective-permute-start.3 = (bf16[2,64,1792]{2,1,0:T(8,128)(2,1)S(1)}, bf16[2,64,1792]{2,1,0:T(8,128)(2,1)S(1)}, u32[]{:S(2)}, u32[]{:S(2)}) collective-permute-start(bf16[2,64,1792]{2,1,0:T(8,128)(2,1)S(1)} %get-tuple-element.23.own_ref), channel_id=1, source_target_pairs={{0,4},{4,0},{8,12},{12,8},{16,20},{20,16},{24,28},{28,24},{1,5},{5... | collective-permute-start | bytes 1376264 | tf_op jit(solution)/shard_map/ppermute | solution.py:394
  28.1 15.1 %collective-permute-start.4 = (bf16[2,64,1792]{2,1,0:T(8,128)(2,1)S(1)}, bf16[2,64,1792]{2,1,0:T(8,128)(2,1)S(1)}, u32[]{:S(2)}, u32[]{:S(2)}) collective-permute-start(bf16[2,64,1792]{2,1,0:T(8,128)(2,1)S(1)} %get-tuple-element.23.own_ref), channel_id=1, source_target_pairs={{4,8},{8,4},{12,16},{16,12},{20,24},{24,20},{5,9},{9,5},{13,17},{1... | collective-permute-start | bytes 1376264 | tf_op jit(solution)/shard_map/ppermute | solution.py:394
  43.2 1.0 %copy-start.13 = (bf16[2,64,1792]{2,1,0:T(8,128)(2,1)S(1)}, bf16[2,64,1792]{2,1,0:T(8,128)(2,1)}, u32[]{:S(2)}) copy-start(bf16[2,64,1792]{2,1,0:T(8,128)(2,1)} %copy-done.12) | copy-start | bytes 1376260
  44.2 0.9 %copy-start.15 = (f32[2,8,2304]{2,1,0:T(8,128)S(1)}, f32[2,8,2304]{2,1,0:T(8,128)}, u32[]{:S(2)}) copy-start(f32[2,8,2304]{2,1,0:T(8,128)} %copy-done.14) | copy-start | bytes 442372
  50.5 3.3 %collective-permute-start.5 = (bf16[2,64,1024]{2,1,0:T(8,128)(2,1)S(1)}, bf16[2,64,1024]{2,1,0:T(8,128)(2,1)S(1)}, u32[]{:S(2)}, u32[]{:S(2)}) collective-permute-start(bf16[2,64,1024]{2,1,0:T(8,128)(2,1)S(1)} %get-tuple-element.27.own_ref), channel_id=1, source_target_pairs={{0,4},{4,0},{8,12},{12,8},{16,20},{20,16},{24,28},{28,24},{1,5},{5... | collective-permute-start | bytes 786440 | tf_op jit(solution)/shard_map/ppermute | solution.py:394
  50.5 10.0 %collective-permute-start.6 = (bf16[2,64,1024]{2,1,0:T(8,128)(2,1)S(1)}, bf16[2,64,1024]{2,1,0:T(8,128)(2,1)S(1)}, u32[]{:S(2)}, u32[]{:S(2)}) collective-permute-start(bf16[2,64,1024]{2,1,0:T(8,128)(2,1)S(1)} %get-tuple-element.27.own_ref), channel_id=1, source_target_pairs={{4,8},{8,4},{12,16},{16,12},{20,24},{24,20},{5,9},{9,5},{13,17},{1... | collective-permute-start | bytes 786440 | tf_op jit(solution)/shard_map/ppermute | solution.py:394

commit v2 on v1

v2 whole, which is shorter than its diff:
```python
import functools
import math

import jax
import jax.numpy as jnp
from jax import lax
from jax.experimental import pallas as pl
from jax.experimental.pallas import tpu as pltpu
from jax.sharding import PartitionSpec as P


F32 = jnp.float32
BF16 = jnp.bfloat16
LANES = 128
BLOCK = 256
FRONT = 2 * LANES
AUG = 8
LAYERS = 3


class Geometry:
    def __init__(self, cells, blocks):
        self.tile = math.isqrt(cells)
        self.halo = LAYERS * blocks
        self.side = self.tile + 2 * self.halo
        self.blocks = blocks
        body = -(-self.side * self.side // BLOCK) * BLOCK
        self.body = body
        self.width = FRONT + body + LANES
        self.strip = self.halo * self.tile

    def lane(self, row, col):
        return FRONT + row * self.side + col

    def span(self, margin):
        first = self.lane(margin, margin)
        last = self.lane(self.side - 1 - margin, self.side - 1 - margin)
        return first // LANES * LANES, (last // LANES + 1) * LANES


def whole():
    return pl.BlockSpec(memory_space=pltpu.VMEM)


def hbm():
    return pl.BlockSpec(memory_space=pltpu.HBM)


def keep_in_hbm(x):
    return pltpu.with_memory_space_constraint(x, pltpu.HBM)


def params(mib=8):
    return pltpu.CompilerParams(vmem_limit_bytes=mib << 20)


def cost(flops, moved=1 << 20):
    return pl.CostEstimate(flops=flops, bytes_accessed=moved, transcendentals=0)


def iota(shape, dim):
    return lax.broadcasted_iota(jnp.int32, shape, dim)


def one_hot(condition):
    return jnp.where(condition, 1.0, 0.0).astype(BF16)


def dot(a, b):
    return jnp.dot(a, b, preferred_element_type=F32)


KIND = (0, 0, 0, 2, 3, 1, 1, 1)


def pack_kernel(g, slots, planes, nbr_hbm, counts_hbm, acts_hbm, mask_hbm, *refs):
    out_refs, (aug_ref, strip_ref, acts_ref, mask_ref, nbr_ref, counts_ref, sems) = refs[:planes], refs[planes:]
    copies = [
        pltpu.make_async_copy(source, target, sems.at[at])
        for at, (source, target) in enumerate(
            ((acts_hbm, acts_ref), (mask_hbm, mask_ref), (nbr_hbm, nbr_ref), (counts_hbm, counts_ref))
        )
    ]
    for copy in copies:
        copy.start()
    me = lax.axis_index("plane")
    tile, halo = g.tile, g.halo
    cells = tile * tile
    rows = acts_ref.shape[2]
    half = LANES // 2
    lane = iota((cells, 2 * LANES), 1)
    lane = jnp.where(lane >= LANES + half, lane - half, lane)
    source = iota((cells, 2 * LANES), 0)
    row, col = source // tile, source % tile
    left = one_hot((row * halo + col == lane) & (col < halo))
    right = one_hot((row * halo + col - (tile - halo) == lane) & (col >= tile - halo))
    i, j = iota((LANES, LANES), 0), iota((LANES, LANES), 1)
    low = one_hot(i == j % half)
    high = one_hot(i == half + j % half)
    for copy in copies:
        copy.wait()
    for a in range(slots):
        alive = a < counts_ref[me]
        aug_ref[a, :rows] = jnp.where(alive, acts_ref[a, 0].astype(F32), 0.0).astype(BF16)
        line = mask_ref[a, 0:1].astype(F32)
        aug_ref[a, rows:] = jnp.where(iota((AUG, cells), 0) == 0, line, 0.0).astype(BF16)
        x = aug_ref[a]
        strip_ref[a, 0, 0] = x[:, :LANES]
        strip_ref[a, 0, 1] = dot(x[:, LANES : 2 * LANES], low).astype(BF16)
        strip_ref[a, 1, 0] = x[:, cells - LANES :]
        strip_ref[a, 1, 1] = dot(x[:, cells - 2 * LANES : cells - LANES], high).astype(BF16)
        for kind, pick in ((2, left), (3, right)):
            both = dot(x, pick).astype(BF16)
            strip_ref[a, kind, 0] = both[:, :LANES]
            strip_ref[a, kind, 1] = both[:, LANES:]
    lower = iota((rows + AUG, LANES), 1) < half
    for k in range(planes):
        peer = partner(me, k, planes, True)
        for a in range(slots):
            kinds = []
            for b in range(slots):
                kind = jnp.int32(0)
                for d in range(8):
                    kind = jnp.where(nbr_ref[a, d] == peer * slots + b, KIND[d], kind)
                kinds.append(kind)
                out_refs[k][slots * a + b] = strip_ref[a, kind, 0]
            out_refs[k][slots * slots + a] = jnp.where(lower, strip_ref[a, kinds[0], 1], strip_ref[a, kinds[1], 1])


def partner(me, k, planes, outgoing):
    if planes & (planes - 1) == 0:
        return me ^ k
    return lax.rem(me + (k if outgoing else planes - k), planes)


def route(me, other, planes):
    if planes & (planes - 1) == 0:
        return me ^ other
    return lax.rem(me - other + planes, planes)


def halo_pieces(g):
    tile, halo, side = g.tile, g.halo, g.side
    pieces = []
    for d in (0, 1, 2, 5, 6, 7):
        first_row = 0 if d < 3 else halo + tile
        cols = {0: (0, halo), 1: (halo, halo + tile), 2: (halo + tile, side)}[d % 3 if d < 3 else (d - 5)]
        blocks = sorted({((first_row + r) * side + c) // BLOCK for r in range(halo) for c in range(*cols)})
        pieces += [(d, n) for n in blocks]
    sides = []
    for part in (0, 1):
        blocks = set()
        for r in range(tile):
            for c in range(halo):
                if (r * halo + c >= LANES) == bool(part):
                    blocks.add(((halo + r) * side + c) // BLOCK)
                    blocks.add(((halo + r) * side + halo + tile + c) // BLOCK)
        sides += [(part, n) for n in sorted(blocks)]
    return pieces, sides


def strip_entry(lane, b, half):
    rest = lane - LANES
    ours = (rest >= b * half) & (rest < (b + 1) * half)
    return jnp.where(lane < LANES, lane, jnp.where(ours, LANES + rest - b * half, -10000))


def own_band(g):
    pairs = set()
    for r in range(g.tile):
        for c in range(g.tile):
            pairs.add(((r * g.tile + c) // BLOCK, ((r + g.halo) * g.side + c + g.halo) // BLOCK))
    return sorted(pairs)


def prepare_kernel(
    g,
    slots,
    aug_ref,
    nbr_hbm,
    weight_hbm,
    bias_hbm,
    dweight_hbm,
    dbias_hbm,
    own_ref,
    pick_ref,
    keep_ref,
    table_ref,
    weight_ref,
    bias_ref,
    dweight_ref,
    raw_weight_ref,
    raw_bias_ref,
    raw_dweight_ref,
    raw_dbias_ref,
    sems,
):
    copies = [
        pltpu.make_async_copy(source, target, sems.at[at])
        for at, (source, target) in enumerate(
            (
                (weight_hbm, raw_weight_ref),
                (bias_hbm, raw_bias_ref),
                (dweight_hbm, raw_dweight_ref),
                (dbias_hbm, raw_dbias_ref),
                (nbr_hbm, table_ref),
            )
        )
    ]
    for copy in copies:
        copy.start()
    tile, halo, side = g.tile, g.halo, g.side
    rows = aug_ref.shape[1] - AUG
    half = LANES // 2
    src = iota((BLOCK, BLOCK), 0)
    dst = iota((BLOCK, BLOCK), 1)
    pairs = own_band(g)
    for n in range(g.body // BLOCK):
        total = [jnp.zeros((rows + AUG, BLOCK), F32) for _ in range(slots)]
        for k in [k for k, m in pairs if m == n]:
            cell = src + k * BLOCK
            where = (cell // tile + halo) * side + cell % tile + halo
            move = one_hot(where == dst + n * BLOCK)
            for a in range(slots):
                total[a] += dot(aug_ref[a, :, k * BLOCK : (k + 1) * BLOCK], move)
        for a in range(slots):
            own_ref[a, :, n * BLOCK : (n + 1) * BLOCK] = total[a].astype(BF16)
    pieces, sides = halo_pieces(g)
    at = 0
    for d, n in pieces:
        for b in range(slots):
            e = strip_entry(src, b, half)
            if d < 3:
                lead = g.strip - LANES
                e = jnp.where(src < LANES, src + lead, e - LANES)
                row, col, base = e // tile, e % tile, 0
            else:
                row, col, base = e // tile, e % tile, halo + tile
            kind = d if d < 3 else d - 5
            if kind == 0:
                good, shift = col >= tile - halo, halo - tile
            elif kind == 1:
                good, shift = col >= 0, halo
            else:
                good, shift = col < halo, halo + tile
            where = (base + row) * side + col + shift
            pick_ref[at] = one_hot((where == dst + n * BLOCK) & good & (e >= 0))
            at += 1
    for part, n in sides:
        for b in range(slots):
            lane = jnp.where(src < LANES, src, src - LANES) + part * LANES
            e = strip_entry(lane, b, half)
            row, col = e // halo, e % halo
            where = (halo + row) * side + col + jnp.where(src < LANES, 0, halo + tile)
            pick_ref[at] = one_hot((where == dst + n * BLOCK) & (e >= 0))
            at += 1
    start, _ = g.span(halo)
    for m, (n, k) in enumerate(keep_band(g)):
        cell = dst + n * BLOCK
        where = FRONT + (cell // tile + halo) * side + cell % tile + halo - start
        keep_ref[m] = one_hot(where == src + k * BLOCK)
    for copy in copies:
        copy.wait()
    odd = lax.rem(lax.axis_index("depth"), 2)
    diagonal = iota((rows, rows), 0) == iota((rows, rows), 1)

    def column(line):
        return jnp.sum(jnp.where(diagonal, line, 0.0), axis=1, keepdims=True)

    for block in range(g.blocks):
        for layer in range(LAYERS):
            for at, row in enumerate((1, 0, 2)):
                piece = raw_weight_ref[block, layer, :, 3 * row * rows : 3 * (row + 1) * rows]
                weight_ref[block, layer, at * rows : (at + 1) * rows] = (0.5 * piece.astype(F32)).astype(BF16)
            bias_ref[block, layer] = 0.5 * column(raw_bias_ref[layer, block : block + 1])
        bias_ref[block, LAYERS] = column(raw_dbias_ref[block : block + 1])
        taps = [raw_dweight_ref[block, :, tap * rows : (tap + 1) * rows].astype(F32) for tap in range(3)]
        dweight_ref[block, 0] = jnp.where(odd == 1, taps[0], taps[2]).astype(BF16)
        dweight_ref[block, 1] = taps[1].astype(BF16)
        dweight_ref[block, 2] = jnp.where(odd == 1, taps[2], taps[0]).astype(BF16)


def keep_band(g):
    start, _ = g.span(g.halo)
    pairs = set()
    for r in range(g.tile):
        for c in range(g.tile):
            pairs.add(((r * g.tile + c) // BLOCK, (g.lane(r + g.halo, c + g.halo) - start) // BLOCK))
    return sorted(pairs)


def conv(g, margin, x_ref, y_ref, stack_ref, middle_ref, outer_ref, weight, bias, mask_ref):
    channels = x_ref.shape[0]
    low, high = g.span(margin - 1)
    start, stop = g.span(margin)
    for col in range(3):
        stack_ref[col * channels : (col + 1) * channels, low:high] = x_ref[:, low + col - 1 : high + col - 1]
    for at in range(low, high, BLOCK):
        lanes = slice(at, min(at + BLOCK, high))
        sums = dot(weight, stack_ref[:, lanes])
        middle_ref[:, lanes] = sums[:channels]
        outer_ref[:, lanes] = sums[channels:]
    for at in range(start, stop, BLOCK):
        end = min(at + BLOCK, stop)
        above = outer_ref[:channels, at - g.side : end - g.side]
        below = outer_ref[channels:, at + g.side : end + g.side]
        half = middle_ref[:, at:end] + bias + above + below
        out = (half + half * jnp.tanh(half)) * mask_ref[0:1, at:end]
        y_ref[:, at:end] = out.astype(BF16)


def branch(g, block, bufs, work, weight_ref, bias_ref, mask_ref):
    for layer in range(LAYERS):
        margin = LAYERS * block + 1 + layer
        source, target = bufs[layer % 2], bufs[(layer + 1) % 2]
        conv(g, margin, source, target, *work, weight_ref[block, layer], bias_ref[block, layer], mask_ref)
    return bufs[LAYERS % 2]


def first_kernel(g, slots, planes, b, table_ref, own_ref, pick_ref, weight_ref, bias_ref, *refs):
    messages = refs[:planes]
    branch_ref, hidden_ref, mask_ref, pool_ref, x_ref, y_ref, *work = refs[planes:]
    me = lax.axis_index("plane")
    channels = weight_ref.shape[2] // 3
    table = table_ref[b : b + 1].astype(F32)
    for k in range(planes):
        for a in range(slots):
            pool_ref[k, a, 0] = messages[k][slots * a + b]
            pool_ref[k, a, 1] = messages[k][slots * slots + a]
    pieces, sides = halo_pieces(g)
    start, stop = g.span(LAYERS)

    def fetch(d):
        source = jnp.sum(jnp.where(iota(table.shape, 1) == d, table, 0.0)).astype(jnp.int32)
        safe = jnp.maximum(source, 0)
        k = route(me, safe // slots, planes)
        a = safe % slots
        ok = source >= 0
        main = pool_ref[k, a, 0]
        rest = pool_ref[k, a, 1]
        main = jnp.where(ok, main.astype(F32), 0.0).astype(BF16)
        rest = jnp.where(ok, rest.astype(F32), 0.0).astype(BF16)
        return main, rest

    strips = {d: fetch(d) for d in range(8)}
    lines = {d: jnp.concatenate(strips[d], axis=1) for d in (0, 1, 2, 5, 6, 7)}
    walls = [jnp.concatenate([strips[3][part], strips[4][part]], axis=1) for part in (0, 1)]
    for n in range(g.body // BLOCK):
        total = own_ref[b, :, n * BLOCK : (n + 1) * BLOCK].astype(F32)
        for at, (d, m) in enumerate(pieces):
            if m == n:
                total += dot(lines[d], pick_ref[at * slots + b])
        for at, (part, m) in enumerate(sides):
            if m == n:
                total += dot(walls[part], pick_ref[(len(pieces) + at) * slots + b])
        lanes = slice(FRONT + n * BLOCK, FRONT + (n + 1) * BLOCK)
        x_ref[:, lanes] = total[:channels].astype(BF16)
        mask_ref[:, lanes] = total[channels:]
    x_ref[:, :FRONT] = jnp.zeros((channels, FRONT), BF16)
    x_ref[:, FRONT + g.body :] = jnp.zeros((channels, LANES), BF16)
    y_ref[...] = jnp.zeros(y_ref.shape, BF16)
    hidden_ref[...] = x_ref[:, start:stop]
    out = branch(g, 0, (x_ref, y_ref), work, weight_ref, bias_ref, mask_ref)
    branch_ref[...] = out[:, start:stop]


def depth_sum(block, bias_ref, weight_ref, own, pair, other):
    total = dot(weight_ref[block, 1], own)
    total += dot(weight_ref[block, 0], pair)
    total += dot(weight_ref[block, 2], other)
    return total + bias_ref[block, LAYERS]


def second_kernel(
    g,
    own_ref,
    pair_ref,
    other_ref,
    hidden_ref,
    mask_ref,
    keep_ref,
    weight_ref,
    bias_ref,
    dweight_ref,
    branch_ref,
    kept_ref,
    x_ref,
    y_ref,
    *work,
):
    start, stop = g.span(LAYERS)
    inner, _ = g.span(g.halo)
    band = keep_band(g)
    cells = g.tile * g.tile

    def keep(buf, ref):
        for n in range(cells // BLOCK):
            total = None
            for m, (i, k) in enumerate(band):
                if i == n:
                    lo = inner + k * BLOCK
                    term = dot(buf[:, lo : lo + BLOCK], keep_ref[m])
                    total = term if total is None else total + term
            ref[:, n * BLOCK : (n + 1) * BLOCK] = total.astype(BF16)

    x_ref[:, :start] = jnp.zeros((x_ref.shape[0], start), BF16)
    x_ref[:, stop:] = jnp.zeros((x_ref.shape[0], x_ref.shape[1] - stop), BF16)
    y_ref[...] = jnp.zeros(y_ref.shape, BF16)
    for at in range(0, stop - start, BLOCK):
        size = min(BLOCK, stop - start - at)
        piece = slice(at, at + size)
        summed = depth_sum(0, bias_ref, dweight_ref, own_ref[:, piece], pair_ref[:, piece], other_ref[:, piece])
        lanes = slice(start + at, start + at + size)
        x_ref[:, lanes] = (hidden_ref[:, piece].astype(F32) + mask_ref[0:1, lanes] * summed).astype(BF16)
    keep(x_ref, kept_ref)
    out = branch(g, 1, (x_ref, y_ref), work, weight_ref, bias_ref, mask_ref)
    keep(out, branch_ref)


def last_kernel(block, b, own_ref, pair_ref, other_ref, kept_ref, mask_ref, bias_ref, dweight_ref, *refs):
    out_ref = refs[-1]
    channels = out_ref.shape[2]
    summed = depth_sum(block, bias_ref, dweight_ref, own_ref[...], pair_ref[...], other_ref[...])
    mask = mask_ref[b, channels : channels + 1].astype(F32)
    out_ref[0, 0] = (kept_ref[...].astype(F32) + mask * summed).astype(BF16)


def neighbours_in_depth(x):
    count = lax.axis_size("depth")

    def swap(first):
        perm = []
        for i in range(first, count - 1, 2):
            perm += [(i, i + 1), (i + 1, i)]
        return lax.ppermute(x, "depth", perm)

    other = swap(1)
    pair = swap(0)
    return pair, other


def shards(
    activations, plane_weight, plane_bias, depth_weight, depth_bias, counts, neighbours, voxel_mask
):
    slots, sections, channels, cells = activations.shape
    blocks = plane_weight.shape[0]
    planes = lax.axis_size("plane")
    assert slots == 2 and sections == 1 and blocks == 2
    g = Geometry(cells, blocks)
    rows = channels + AUG
    message = jax.ShapeDtypeStruct((slots * slots + slots, rows, LANES), BF16)
    aug_shape = jax.ShapeDtypeStruct((slots, rows, cells), BF16)
    *packed, aug = pl.pallas_call(
        functools.partial(pack_kernel, g, slots, planes),
        out_shape=[message] * planes + [aug_shape],
        in_specs=[hbm()] * 4,
        out_specs=[whole()] * (planes + 1),
        scratch_shapes=[
            pltpu.VMEM((slots, 4, 2, rows, LANES), BF16),
            pltpu.VMEM(activations.shape, BF16),
            pltpu.VMEM(voxel_mask.shape, jnp.int32),
            pltpu.SMEM(neighbours.shape, jnp.int32),
            pltpu.SMEM(counts.shape, jnp.int32),
            pltpu.SemaphoreType.DMA((4,)),
        ],
        compiler_params=params(),
        cost_estimate=cost(1 << 28),
        name="pack",
    )(*map(keep_in_hbm, (neighbours, counts, activations, voxel_mask)))
    received = [packed[0]] + [None] * (planes - 1)
    for k in reversed(range(1, planes)):
        if planes & (planes - 1) == 0:
            perm = [(i, i ^ k) for i in range(planes)]
        else:
            perm = [(i, (i + k) % planes) for i in range(planes)]
        received[k] = lax.ppermute(packed[k], "plane", perm)

    pieces, sides = halo_pieces(g)
    own, pick, keep, table, weight, bias, dweight = pl.pallas_call(
        functools.partial(prepare_kernel, g, slots),
        out_shape=[
            jax.ShapeDtypeStruct((slots, rows, g.body), BF16),
            jax.ShapeDtypeStruct(((len(pieces) + len(sides)) * slots, BLOCK, BLOCK), BF16),
            jax.ShapeDtypeStruct((len(keep_band(g)), BLOCK, BLOCK), BF16),
            jax.ShapeDtypeStruct(neighbours.shape, jnp.int32),
            jax.ShapeDtypeStruct((blocks, LAYERS, 3 * channels, 3 * channels), BF16),
            jax.ShapeDtypeStruct((blocks, LAYERS + 1, channels, 1), F32),
            jax.ShapeDtypeStruct((blocks, 3, channels, channels), BF16),
        ],
        in_specs=[whole()] + [hbm()] * 5,
        out_specs=[whole()] * 7,
        scratch_shapes=[
            pltpu.VMEM(plane_weight.shape, BF16),
            pltpu.VMEM((LAYERS, blocks, channels), F32),
            pltpu.VMEM(depth_weight.shape, BF16),
            pltpu.VMEM(depth_bias.shape, F32),
            pltpu.SemaphoreType.DMA((5,)),
        ],
        compiler_params=params(),
        cost_estimate=cost(1 << 29),
        name="prepare",
    )(aug, *map(keep_in_hbm, (neighbours, plane_weight, plane_bias.swapaxes(0, 1), depth_weight, depth_bias)))

    start, stop = g.span(LAYERS)
    work = [
        pltpu.VMEM((channels, g.width), BF16),
        pltpu.VMEM((channels, g.width), BF16),
        pltpu.VMEM((3 * channels, g.width), BF16),
        pltpu.VMEM((channels, g.width), F32),
        pltpu.VMEM((2 * channels, g.width), F32),
    ]
    wide = jax.ShapeDtypeStruct((channels, stop - start), BF16)
    narrow = jax.ShapeDtypeStruct((channels, cells), BF16)
    firsts, seconds = [], []
    for b in range(slots):
        branch0, hidden0, mask = pl.pallas_call(
            functools.partial(first_kernel, g, slots, planes, b),
            out_shape=[wide, wide, jax.ShapeDtypeStruct((AUG, g.width), F32)],
            in_specs=[whole()] * (5 + planes),
            out_specs=[whole()] * 3,
            scratch_shapes=[pltpu.VMEM((planes, slots, 2, rows, LANES), BF16)] + work,
            compiler_params=params(10),
            cost_estimate=cost(1 << 30),
        )(table, own, pick, weight, bias, *received)
        firsts.append((branch0, *neighbours_in_depth(branch0), hidden0, mask))
    for b in range(slots):
        branch1, kept = pl.pallas_call(
            functools.partial(second_kernel, g),
            out_shape=[narrow, narrow],
            in_specs=[whole()] * 9,
            out_specs=[whole()] * 2,
            scratch_shapes=work,
            compiler_params=params(10),
            cost_estimate=cost(1 << 30),
        )(*firsts[b], keep, weight, bias, dweight)
        seconds.append((branch1, *neighbours_in_depth(branch1), kept))
    out = None
    for b in range(slots):
        more = [] if out is None else [out]
        out = pl.pallas_call(
            functools.partial(last_kernel, blocks - 1, b),
            out_shape=jax.ShapeDtypeStruct(activations.shape, BF16),
            grid=(1,),
            in_specs=[whole()] * 7 + [hbm()] * len(more),
            out_specs=pl.BlockSpec((1, 1, channels, cells), lambda i, b=b: (b, 0, 0, 0)),
            input_output_aliases={7: 0} if more else {},
            compiler_params=params(),
            cost_estimate=cost(1 << 26),
        )(*seconds[b], aug, bias, dweight, *more)
    return out


def solution(mesh):
    in_specs = (
        P("plane", "depth", None, None),
        P(),
        P(),
        P(),
        P(),
        P(),
        P("plane", None),
        P("plane", "depth", None),
    )
    out_specs = P("plane", "depth", None, None)
    return jax.shard_map(shards, mesh=mesh, in_specs=in_specs, out_specs=out_specs, check_vma=False)
```

time: 62.7 us -> 44.6 us (0.71)
  local copies, waits for them, and re-layouts: 13 us -> 0 us
  waiting for transfers between devices: 18.8 us -> 7.69 us
  starting transfers between devices: 13.1 us -> 20.7 us
  Pallas kernels: 16.5 us -> 15.3 us
    ppermute x4 -> x8, waiting for transfers between devices: 17.4 us -> 2.41 us  [swap(): return lax.ppermute(x, 'depth', perm)]
    unnamed x35 -> x0, local copies, waits for them, and re-layouts: 12 us -> none
    ppermute x4 -> x8, starting transfers between devices: 9.45 us -> 17 us  [swap(): return lax.ppermute(x, 'depth', perm)]
    ppermute x3, waiting for transfers between devices: 1.4 us -> 5.28 us  [shards(): received[k] = lax.ppermute(packed[k], 'plane', perm)]
    pallas_call x3 -> x6, Pallas kernels: 13.5 us -> 11.8 us  [the longest x2 5.14 us: shards(): pl.pallas_call(functools.partial(first_kernel, g, slots, planes, b), out_...]
    broadcast_in_dim x2 -> x0, local copies, waits for them, and re-layouts: 0.91 us -> none  [the longest x1 0.81 us: shards(): bias = plane_bias[..., None]]
  transfers between devices with their start and end apart: 7 -> 11, of which waited for: 3 -> 3; matrix products, arithmetic and copies ran while one was open for 3% -> 0% of each run, Pallas kernels for 3% -> 23%
where the time goes in v2:
time: 44.6 us; the launch traced here: 43.8 us
  starting transfers between devices  20.7 us (46%)
  Pallas kernels  15.3 us (34%)
  waiting for transfers between devices  7.69 us (17%)
    ppermute x8, starting transfers between devices, swap(): return lax.ppermute(x, 'depth', perm)  17 us
    ppermute x3, waiting for transfers between devices, shards(): received[k] = lax.ppermute(packed[k], 'plane', perm)  5.28 us
    pallas_call x2, Pallas kernels, shards(): pl.pallas_call(functools.partial(first_kernel, g, slots, planes, b), out_...  5.14 us
    pallas_call x2, Pallas kernels, shards(): pl.pallas_call(functools.partial(second_kernel, g), out_shape=[narrow, na...  4.87 us
    ppermute x3, starting transfers between devices, shards(): received[k] = lax.ppermute(packed[k], 'plane', perm)  3.67 us
    ppermute x8, waiting for transfers between devices, swap(): return lax.ppermute(x, 'depth', perm)  2.41 us
    pallas_call x2, Pallas kernels, shards(): pl.pallas_call(functools.partial(last_kernel, blocks - 1, b), out_shape=j...  1.84 us
    pallas_call x1, Pallas kernels, shards(): pl.pallas_call(functools.partial(prepare_kernel, g, slots), out_shape=[ja...  1.84 us
  transfers between devices with their start and end apart: 11, of which 3 were waited for; matrix products, arithmetic and copies ran while one was open for 0% of the time, Pallas kernels for 23%

profile of v2, /device:TPU:3, one launch (start us, length us, event | category | flops | bytes accessed | tf_op | source)
XLA Modules:
  0.0 43.8 jit_solution(13772267394926048878)
XLA Ops:
  0.0 1.6 %pack.1 = (bf16[6,72,128]{2,1,0:T(8,128)(2,1)S(1)}, bf16[6,72,128]{2,1,0:T(8,128)(2,1)S(1)}, bf16[6,72,128]{2,1,0:T(8,128)(2,1)S(1)}, bf16[6,72,128]{2,1,0:T(8,128)(2,1)S(1)}, bf16[2,72,1024]{2,1,0:T(8,128)(2,1)S(1)}) custom-call(s32[2,8]{1,0:T(2,128)} %nbr_hbm.3, s32[4]{0:T(128)} %counts_hbm.1, bf16[2,1,64,1024]{3,2,1,0:T(8,128)(2,1)} %acts_hbm.1, ...), custom_call_target="tpu_custom_call" | custom-call | flops 268435456 | bytes 1048576 | tf_op jit(solution)/shard_map/pack/pallas_call | solution.py:453
  1.6 1.4 %collective-permute-start = (bf16[6,72,128]{2,1,0:T(8,128)(2,1)S(1)}, bf16[6,72,128]{2,1,0:T(8,128)(2,1)S(1)}, u32[]{:S(2)}, u32[]{:S(2)}) collective-permute-start(bf16[6,72,128]{2,1,0:T(8,128)(2,1)S(1)} %get-tuple-element.34), channel_id=1, source_target_pairs={{0,1},{1,0},{2,3},{3,2},{4,5},{5,4},{6,7},{7,6},{8,9},{9,8},{10,11... | collective-permute-start | bytes 331784 | tf_op jit(solution)/shard_map/ppermute | solution.py:476
  3.0 2.3 %collective-permute-start.1 = (bf16[6,72,128]{2,1,0:T(8,128)(2,1)S(1)}, bf16[6,72,128]{2,1,0:T(8,128)(2,1)S(1)}, u32[]{:S(2)}, u32[]{:S(2)}) collective-permute-start(bf16[6,72,128]{2,1,0:T(8,128)(2,1)S(1)} %get-tuple-element.35), channel_id=1, source_target_pairs={{0,2},{1,3},{2,0},{3,1},{4,6},{5,7},{6,4},{7,5},{8,10},{9,11},{10,... | collective-permute-start | bytes 331784 | tf_op jit(solution)/shard_map/ppermute | solution.py:476
  5.3 1.8 %prepare.1 = (bf16[2,72,2048]{2,1,0:T(8,128)(2,1)S(1)}, bf16[36,256,256]{2,1,0:T(8,128)(2,1)S(1)}, bf16[9,256,256]{2,1,0:T(8,128)(2,1)S(1)}, s32[2,8]{1,0:T(2,12...) custom-call(bf16[2,72,1024]{2,1,0:T(8,128)(2,1)S(1)} %get-tuple-elemen, ...), custom_call_target="tpu_custom_call" | custom-call | flops 536870912 | bytes 1048576 | tf_op jit(solution)/shard_map/prepare/pallas_call | solution.py:479
  7.1 0.0 collective-permute-done.refs_1_
  7.1 0.5 %collective-permute-done.1.refs_2_ = bf16[6,72,128]{2,1,0:T(8,128)(2,1)S(1)} collective-permute-done((bf16[6,72,128]{2,1,0:T(8,128)(2,1)S(1)}, bf16[6,72,128]{2,1,0:T(8,128)(2,1)S(1)}, u32[]{:S(2)}, u32[]{:S(2)}) %collective-permute-start.1) | collective-permute-done | bytes 110624 | tf_op jit(solution)/shard_map/ppermute | solution.py:476
  7.7 4.7 %collective-permute-done.2.refs_3_ = bf16[6,72,128]{2,1,0:T(8,128)(2,1)S(1)} collective-permute-done((bf16[6,72,128]{2,1,0:T(8,128)(2,1)S(1)}, bf16[6,72,128]{2,1,0:T(8,128)(2,1)S(1)}, u32[]{:S(2)}, u32[]{:S(2)}) %collective-permute-start.2) | collective-permute-done | bytes 110624 | tf_op jit(solution)/shard_map/ppermute | solution.py:476
  12.4 2.6 %shard_map.84 = (bf16[64,1792]{1,0:T(8,128)(2,1)S(1)}, bf16[64,1792]{1,0:T(8,128)(2,1)S(1)}, f32[8,2432]{1,0:T(8,128)S(1)}) custom-call(s32[2,8]{1,0:T(2,128)S(1)} %get-tuple-element.28.table_ref, bf16[2,72,2048]{2,1,0:T(8,128)(2,1)S(1)} %get-tuple-element.29.own_ref, bf16[36,256,256]{2,1,0:T(8,128)(2,1)S(1)} %get-tuple-element.30.pick_ref, ...), custom_call_target="tpu_custom_call" | custom-call | flops 1073741824 | bytes 1048576 | tf_op jit(solution)/shard_map/pallas_call | solution.py:516
  15.0 5.9 %collective-permute-start.8 = (bf16[64,1792]{1,0:T(8,128)(2,1)S(1)}, bf16[64,1792]{1,0:T(8,128)(2,1)S(1)}, u32[]{:S(2)}, u32[]{:S(2)}) collective-permute-start(bf16[64,1792]{1,0:T(8,128)(2,1)S(1)} %get-tuple-element.44.own_ref), channel_id=1, source_target_pairs={{4,8},{8,4},{12,16},{16,12},{20,24},{24,20},{5,9},{9,5},{13,17},{1... | collective-permute-start | bytes 688136 | tf_op jit(solution)/shard_map/ppermute | solution.py:435
  20.9 0.1 collective-permute-start.7
  21.0 2.6 %shard_map.82 = (bf16[64,1792]{1,0:T(8,128)(2,1)S(1)}, bf16[64,1792]{1,0:T(8,128)(2,1)S(1)}, f32[8,2432]{1,0:T(8,128)S(1)}) custom-call(s32[2,8]{1,0:T(2,128)S(1)} %get-tuple-element.28.table_ref, bf16[2,72,2048]{2,1,0:T(8,128)(2,1)S(1)} %get-tuple-element.29.own_ref, bf16[36,256,256]{2,1,0:T(8,128)(2,1)S(1)} %get-tuple-element.30.pick_ref, ...), custom_call_target="tpu_custom_call" | custom-call | flops 1073741824 | bytes 1048576 | tf_op jit(solution)/shard_map/pallas_call | solution.py:516
  23.6 3.5 %collective-permute-start.4 = (bf16[64,1792]{1,0:T(8,128)(2,1)S(1)}, bf16[64,1792]{1,0:T(8,128)(2,1)S(1)}, u32[]{:S(2)}, u32[]{:S(2)}) collective-permute-start(bf16[64,1792]{1,0:T(8,128)(2,1)S(1)} %get-tuple-element.37.own_ref), channel_id=1, source_target_pairs={{4,8},{8,4},{12,16},{16,12},{20,24},{24,20},{5,9},{9,5},{13,17},{1... | collective-permute-start | bytes 688136 | tf_op jit(solution)/shard_map/ppermute | solution.py:435
  27.1 0.1 collective-permute-start.3
  27.2 0.0 collective-permute-done.7.pair_ref
  27.2 2.4 %shard_map.85 = (bf16[64,1024]{1,0:T(8,128)(2,1)S(1)}, bf16[64,1024]{1,0:T(8,128)(2,1)S(1)}) custom-call(bf16[64,1792]{1,0:T(8,128)(2,1)S(1)} %get-tuple-element.44.own_ref, bf16[64,1792]{1,0:T(8,128)(2,1)S(1)} %collective-permute-done.7.pair_ref, bf16[64,1792]{1,0:T(8,128)(2,1)S(1)} %collective-permute-done.8.other_ref, ...), custom_call_target="tpu_custom_call" | custom-call | flops 1073741824 | bytes 1048576 | tf_op jit(solution)/shard_map/pallas_call | solution.py:527
  29.6 3.5 %collective-permute-start.10 = (bf16[64,1024]{1,0:T(8,128)(2,1)S(1)}, bf16[64,1024]{1,0:T(8,128)(2,1)S(1)}, u32[]{:S(2)}, u32[]{:S(2)}) collective-permute-start(bf16[64,1024]{1,0:T(8,128)(2,1)S(1)} %get-tuple-element.47.own_ref), channel_id=1, source_target_pairs={{4,8},{8,4},{12,16},{16,12},{20,24},{24,20},{5,9},{9,5},{13,17},{1... | collective-permute-start | bytes 393224 | tf_op jit(solution)/shard_map/ppermute | solution.py:435
  33.1 0.1 collective-permute-start.9
  33.2 0.0 collective-permute-done.4.other_ref
  33.2 2.4 %shard_map.83 = (bf16[64,1024]{1,0:T(8,128)(2,1)S(1)}, bf16[64,1024]{1,0:T(8,128)(2,1)S(1)}) custom-call(bf16[64,1792]{1,0:T(8,128)(2,1)S(1)} %get-tuple-element.37.own_ref, bf16[64,1792]{1,0:T(8,128)(2,1)S(1)} %collective-permute-done.3.pair_ref, bf16[64,1792]{1,0:T(8,128)(2,1)S(1)} %collective-permute-done.4.other_ref, ...), custom_call_target="tpu_custom_call" | custom-call | flops 1073741824 | bytes 1048576 | tf_op jit(solution)/shard_map/pallas_call | solution.py:527
  35.7 3.8 %collective-permute-start.6 = (bf16[64,1024]{1,0:T(8,128)(2,1)S(1)}, bf16[64,1024]{1,0:T(8,128)(2,1)S(1)}, u32[]{:S(2)}, u32[]{:S(2)}) collective-permute-start(bf16[64,1024]{1,0:T(8,128)(2,1)S(1)} %get-tuple-element.42.own_ref), channel_id=1, source_target_pairs={{4,8},{8,4},{12,16},{16,12},{20,24},{24,20},{5,9},{9,5},{13,17},{1... | collective-permute-start | bytes 393224 | tf_op jit(solution)/shard_map/ppermute | solution.py:435
  39.5 0.1 collective-permute-start.5
  39.6 0.9 %shard_map.86.refs_0_ = bf16[2,1,64,1024]{3,2,1,0:T(8,128)(2,1)} custom-call(bf16[64,1024]{1,0:T(8,128)(2,1)S(1)} %get-tuple-element.47.own_ref, bf16[64,1024]{1,0:T(8,128)(2,1)S(1)} %collective-permute-done.9.pair_ref, bf16[64,1024]{1,0:T(8,128)(2,1)S(1)} %collective-permute-done.10.other_ref, bf16[64,1024]{1,0:T(8,128)(2,1)S(1)} %get-tuple-element.48.kept_ref, ...), custom_call_target="tpu_custom_call" | custom-call | flops 67108864 | bytes 1048576 | tf_op jit(solution)/shard_map/pallas_call | solution.py:540
  40.5 2.4 %collective-permute-done.6.other_ref = bf16[64,1024]{1,0:T(8,128)(2,1)S(1)} collective-permute-done((bf16[64,1024]{1,0:T(8,128)(2,1)S(1)}, bf16[64,1024]{1,0:T(8,128)(2,1)S(1)}, u32[]{:S(2)}, u32[]{:S(2)}) %collective-permute-start.6) | collective-permute-done | bytes 131104 | tf_op jit(solution)/shard_map/ppermute | solution.py:435
  42.9 0.9 %shard_map.87 = bf16[2,1,64,1024]{3,2,1,0:T(8,128)(2,1)} custom-call(bf16[64,1024]{1,0:T(8,128)(2,1)S(1)} %get-tuple-element.42.own_ref, bf16[64,1024]{1,0:T(8,128)(2,1)S(1)} %collective-permute-done.5.pair_ref, bf16[64,1024]{1,0:T(8,128)(2,1)S(1)} %collective-permute-done.6.other_ref, ...), custom_call_target="tpu_custom_call", output_to_operand_aliasing={{}: (7, {})} | custom-call | flops 67108864 | bytes 1048576 | tf_op jit(solution)/shard_map/pallas_call | solution.py:540
  (6 shorter events, 0.0 us)
Async XLA Ops:
  1.6 5.5 %collective-permute-start = (bf16[6,72,128]{2,1,0:T(8,128)(2,1)S(1)}, bf16[6,72,128]{2,1,0:T(8,128)(2,1)S(1)}, u32[]{:S(2)}, u32[]{:S(2)}) collective-permute-start(bf16[6,72,128]{2,1,0:T(8,128)(2,1)S(1)} %get-tuple-element.34), channel_id=1, source_target_pairs={{0,1},{1,0},{2,3},{3,2},{4,5},{5,4},{6,7},{7,6},{8,9},{9,8},{10,11... | collective-permute-start | bytes 331784 | tf_op jit(solution)/shard_map/ppermute | solution.py:476
  3.0 4.7 %collective-permute-start.1 = (bf16[6,72,128]{2,1,0:T(8,128)(2,1)S(1)}, bf16[6,72,128]{2,1,0:T(8,128)(2,1)S(1)}, u32[]{:S(2)}, u32[]{:S(2)}) collective-permute-start(bf16[6,72,128]{2,1,0:T(8,128)(2,1)S(1)} %get-tuple-element.35), channel_id=1, source_target_pairs={{0,2},{1,3},{2,0},{3,1},{4,6},{5,7},{6,4},{7,5},{8,10},{9,11},{10,... | collective-permute-start | bytes 331784 | tf_op jit(solution)/shard_map/ppermute | solution.py:476
  5.3 7.1 %collective-permute-start.2 = (bf16[6,72,128]{2,1,0:T(8,128)(2,1)S(1)}, bf16[6,72,128]{2,1,0:T(8,128)(2,1)S(1)}, u32[]{:S(2)}, u32[]{:S(2)}) collective-permute-start(bf16[6,72,128]{2,1,0:T(8,128)(2,1)S(1)} %get-tuple-element.36), channel_id=1, source_target_pairs={{0,3},{1,2},{2,1},{3,0},{4,7},{5,6},{6,5},{7,4},{8,11},{9,10},{10,... | collective-permute-start | bytes 331784 | tf_op jit(solution)/shard_map/ppermute | solution.py:476
  15.0 12.2 %collective-permute-start.8 = (bf16[64,1792]{1,0:T(8,128)(2,1)S(1)}, bf16[64,1792]{1,0:T(8,128)(2,1)S(1)}, u32[]{:S(2)}, u32[]{:S(2)}) collective-permute-start(bf16[64,1792]{1,0:T(8,128)(2,1)S(1)} %get-tuple-element.44.own_ref), channel_id=1, source_target_pairs={{4,8},{8,4},{12,16},{16,12},{20,24},{24,20},{5,9},{9,5},{13,17},{1... | collective-permute-start | bytes 688136 | tf_op jit(solution)/shard_map/ppermute | solution.py:435
  20.9 6.3 %collective-permute-start.7 = (bf16[64,1792]{1,0:T(8,128)(2,1)S(1)}, bf16[64,1792]{1,0:T(8,128)(2,1)S(1)}, u32[]{:S(2)}, u32[]{:S(2)}) collective-permute-start(bf16[64,1792]{1,0:T(8,128)(2,1)S(1)} %get-tuple-element.44.own_ref), channel_id=1, source_target_pairs={{0,4},{4,0},{8,12},{12,8},{16,20},{20,16},{24,28},{28,24},{1,5},{5... | collective-permute-start | bytes 688136 | tf_op jit(solution)/shard_map/ppermute | solution.py:435
  23.6 9.7 %collective-permute-start.4 = (bf16[64,1792]{1,0:T(8,128)(2,1)S(1)}, bf16[64,1792]{1,0:T(8,128)(2,1)S(1)}, u32[]{:S(2)}, u32[]{:S(2)}) collective-permute-start(bf16[64,1792]{1,0:T(8,128)(2,1)S(1)} %get-tuple-element.37.own_ref), channel_id=1, source_target_pairs={{4,8},{8,4},{12,16},{16,12},{20,24},{24,20},{5,9},{9,5},{13,17},{1... | collective-permute-start | bytes 688136 | tf_op jit(solution)/shard_map/ppermute | solution.py:435
  27.1 6.2 %collective-permute-start.3 = (bf16[64,1792]{1,0:T(8,128)(2,1)S(1)}, bf16[64,1792]{1,0:T(8,128)(2,1)S(1)}, u32[]{:S(2)}, u32[]{:S(2)}) collective-permute-start(bf16[64,1792]{1,0:T(8,128)(2,1)S(1)} %get-tuple-element.37.own_ref), channel_id=1, source_target_pairs={{0,4},{4,0},{8,12},{12,8},{16,20},{20,16},{24,28},{28,24},{1,5},{5... | collective-permute-start | bytes 688136 | tf_op jit(solution)/shard_map/ppermute | solution.py:435
  29.6 9.9 %collective-permute-start.10 = (bf16[64,1024]{1,0:T(8,128)(2,1)S(1)}, bf16[64,1024]{1,0:T(8,128)(2,1)S(1)}, u32[]{:S(2)}, u32[]{:S(2)}) collective-permute-start(bf16[64,1024]{1,0:T(8,128)(2,1)S(1)} %get-tuple-element.47.own_ref), channel_id=1, source_target_pairs={{4,8},{8,4},{12,16},{16,12},{20,24},{24,20},{5,9},{9,5},{13,17},{1... | collective-permute-start | bytes 393224 | tf_op jit(solution)/shard_map/ppermute | solution.py:435
  33.1 6.4 %collective-permute-start.9 = (bf16[64,1024]{1,0:T(8,128)(2,1)S(1)}, bf16[64,1024]{1,0:T(8,128)(2,1)S(1)}, u32[]{:S(2)}, u32[]{:S(2)}) collective-permute-start(bf16[64,1024]{1,0:T(8,128)(2,1)S(1)} %get-tuple-element.47.own_ref), channel_id=1, source_target_pairs={{0,4},{4,0},{8,12},{12,8},{16,20},{20,16},{24,28},{28,24},{1,5},{5... | collective-permute-start | bytes 393224 | tf_op jit(solution)/shard_map/ppermute | solution.py:435
  35.7 7.2 %collective-permute-start.6 = (bf16[64,1024]{1,0:T(8,128)(2,1)S(1)}, bf16[64,1024]{1,0:T(8,128)(2,1)S(1)}, u32[]{:S(2)}, u32[]{:S(2)}) collective-permute-start(bf16[64,1024]{1,0:T(8,128)(2,1)S(1)} %get-tuple-element.42.own_ref), channel_id=1, source_target_pairs={{4,8},{8,4},{12,16},{16,12},{20,24},{24,20},{5,9},{9,5},{13,17},{1... | collective-permute-start | bytes 393224 | tf_op jit(solution)/shard_map/ppermute | solution.py:435
  39.5 3.4 %collective-permute-start.5 = (bf16[64,1024]{1,0:T(8,128)(2,1)S(1)}, bf16[64,1024]{1,0:T(8,128)(2,1)S(1)}, u32[]{:S(2)}, u32[]{:S(2)}) collective-permute-start(bf16[64,1024]{1,0:T(8,128)(2,1)S(1)} %get-tuple-element.42.own_ref), channel_id=1, source_target_pairs={{0,4},{4,0},{8,12},{12,8},{16,20},{20,16},{24,28},{28,24},{1,5},{5... | collective-permute-start | bytes 393224 | tf_op jit(solution)/shard_map/ppermute | solution.py:435
